TPU v7x, 512 devices: a whole 4x8x8 slice. The times are simulated.
512 devices in a mesh: xy: 64 (over y, z_lo, core), gz: 8 (over x, z_hi).
Axes of the slice: x: 4, y: 8, z: 8 (z_hi: 2, z_lo: 4; z = z_hi * 4 + z_lo), core: 2. Of those that a mesh axis runs over, the one named last changes fastest.
Arguments:
- positions: float32 [3, 32, 8, 64, 128], P(None, None, 'gz', 'xy'), may hold values from 0 to 2
- velocities: float32 [3, 32, 8, 64, 128], P(None, None, 'gz', 'xy'), may hold values from -6 to 6
- forces_prev: float32 [3, 32, 8, 64, 128], P(None, None, 'gz', 'xy'), may hold values from -48 to 48
- seeds: int32 [32, 8, 64, 128], P(None, 'gz', 'xy'), may hold values from 0 to 16383
- counts: int32 [8, 64, 128], P('gz', 'xy'), may hold values from 12 to 32, as said below
- offsets: int32 [2], replicated, may hold values from 0 to 127
Outputs:
- forces: float32 [3, 32, 8, 64, 128], P(None, None, 'gz', 'xy')
- velocities_out: float32 [3, 32, 8, 64, 128], P(None, None, 'gz', 'xy')
- stress: float32 [6, 8, 64, 128], P(None, 'gz', 'xy')
Inputs may be any that keep to these rules, and one draw needn't show every extreme that they name: `counts`: each cell holds 12 to 32 beads; every row of 128 cells along x has a full cell.
All inputs are finite; a program needn't handle non-finite values.
Results may differ from a plain program's by a relative error of at most 0.0003.
Values sent between devices are 32-bit elements; how exact they have to be, the bound alone decides.
A program may use at most 128 MiB of HBM per device.

v0:
```python
import math

import jax
import jax.numpy as jnp
from jax import lax
from jax.sharding import PartitionSpec as P

CONSERVATIVE = 25.0
FRICTION = 4.5
NOISE_LEVEL = 3.0
TIME_STEP = 0.04
SHEAR_SPEED = 1.0
CELL_VOLUME = 8.0
FLOOR_SQUARED = 0.0025
COMPONENT_PAIRS = [(0, 0), (1, 1), (2, 2), (0, 1), (0, 2), (1, 2)]
NEIGHBOURS = [(dz, dy, dx) for dz in (-1, 0, 1) for dy in (-1, 0, 1) for dx in (-1, 0, 1)]


def with_halo(block, sides, width):
    for axis, dim in sides:
        count = lax.axis_size(axis)
        forward = [(i, i + 1) for i in range(count - 1)]
        forward.append((count - 1, 0))
        backward = [(target, source) for source, target in forward]
        low = lax.ppermute(
            lax.slice_in_dim(block, block.shape[dim] - width, None, axis=dim), axis, forward
        )
        high = lax.ppermute(lax.slice_in_dim(block, 0, width, axis=dim), axis, backward)
        block = jnp.concatenate([low, block, high], axis=dim)
    return block


def pair_terms(home_beads, near_beads, offset, same_cell, step):
    slots = home_beads.shape[1]
    shift = jnp.asarray([offset[0], offset[1], offset[2]], jnp.float32)[:, None, None, None]
    separation = home_beads[0:3, :, None, :] - near_beads[0:3, None, :, :] - 2.0 * shift
    velocity_gap = home_beads[3:6, :, None, :] - near_beads[3:6, None, :, :]
    squared = jnp.sum(separation * separation, axis=0)
    distance = jnp.sqrt(jnp.maximum(squared, FLOOR_SQUARED))
    occupied = home_beads[7][:, None, :] * near_beads[7][None, :, :]
    if same_cell:
        occupied = occupied * (1.0 - jnp.eye(slots, dtype=jnp.float32))[:, :, None]
    weight = jnp.maximum(1.0 - distance, 0.0) * occupied
    seed_sum = (
        home_beads[6].astype(jnp.int32)[:, None, :]
        + near_beads[6].astype(jnp.int32)[None, :, :]
        + (7919 * step + 1)
    )
    hashed = seed_sum * (seed_sum + 1) % 65521
    noise = (hashed.astype(jnp.float32) / 65521.0 - 0.5) * math.sqrt(12.0)
    approach = jnp.sum(separation * velocity_gap, axis=0) / distance
    magnitude = (
        CONSERVATIVE * weight
        - FRICTION * weight * weight * approach
        + NOISE_LEVEL * weight * noise / math.sqrt(TIME_STEP)
    ) / distance
    pair_force = magnitude[None] * separation
    home_force = jnp.sum(pair_force, axis=2)
    near_force = -jnp.sum(pair_force, axis=1)
    virial = jnp.stack(
        [
            jnp.sum(separation[first] * pair_force[second], axis=(0, 1))
            for first, second in COMPONENT_PAIRS
        ]
    ) * (0.5 / CELL_VOLUME)
    return (home_force, near_force, virial)


def extend(state, offset_now):
    extended = with_halo(state, (("xy", 3), ("gz", 2)), 1)
    index = lax.axis_index("xy")
    count = lax.axis_size("xy")
    shear = jnp.asarray([0.0, 0.0, 0.0, SHEAR_SPEED, 0.0, 0.0, 0.0, 0.0], jnp.float32)[
        :, None, None, None
    ]
    lower = extended[:, :, :, 0, :]
    upper = extended[:, :, :, -1, :]
    lower = jnp.where(index == 0, jnp.roll(lower, -offset_now, axis=-1) - shear, lower)
    upper = jnp.where(index == count - 1, jnp.roll(upper, offset_now, axis=-1) + shear, upper)
    return extended.at[:, :, :, 0, :].set(lower).at[:, :, :, -1, :].set(upper)


def evaluate(state, offset_now, step):
    extended = extend(state, offset_now)
    slots = state.shape[1]
    depth, rows, width = (state.shape[2], state.shape[3], state.shape[4])

    def home_of(level):
        return lax.dynamic_index_in_dim(state, level, 2, keepdims=False).reshape(8, slots, -1)

    def near_of(level, dz, dy, dx):
        plane = lax.dynamic_index_in_dim(extended, level + 1 + dz, 2, keepdims=False)
        block = plane[:, :, 1 + dy : 1 + dy + rows, :]
        return jnp.roll(block, -dx, axis=-1).reshape(8, slots, -1)

    def plane_full(level):
        home = home_of(level)
        plane_force = jnp.zeros((3, slots, rows * width), jnp.float32)
        plane_virial = jnp.zeros((6, rows * width), jnp.float32)
        for dz, dy, dx in NEIGHBOURS:
            same = (dz, dy, dx) == (0, 0, 0)
            home_force, near_force, virial = pair_terms(
                home, near_of(level, dz, dy, dx), (dx, dy, dz), same, step
            )
            plane_force = plane_force + home_force
            plane_virial = plane_virial + virial
        return (plane_force, plane_virial)

    planes_force, planes_virial = lax.map(plane_full, jnp.arange(depth, dtype=jnp.int32))
    total_force = jnp.moveaxis(planes_force, 0, 2).reshape(3, slots, -1)
    total_virial = jnp.moveaxis(planes_virial, 0, 1).reshape(6, -1)
    return (
        total_force.reshape(3, slots, depth, rows, width),
        total_virial.reshape(6, depth, rows, width),
    )


def shards(positions, velocities, forces_prev, seeds, counts, offsets):
    present = (lax.broadcasted_iota(jnp.int32, seeds.shape, 0) < counts[None]).astype(jnp.float32)
    fixed_part = jnp.stack([seeds.astype(jnp.float32), present])
    position_now = positions
    velocity_now = velocities
    force_now = forces_prev
    stress = None
    for step in range(2):
        half_speed = velocity_now + 0.5 * TIME_STEP * force_now
        position_now = position_now + TIME_STEP * half_speed
        state = jnp.concatenate([position_now, half_speed, fixed_part], axis=0)
        force_now, stress = evaluate(state, offsets[step], step)
        velocity_now = half_speed + 0.5 * TIME_STEP * force_now
    return (force_now, velocity_now * present[None], stress)


def solution(mesh):
    placed = (
        P(None, None, "gz", "xy", None),
        P(None, None, "gz", "xy", None),
        P(None, None, "gz", "xy", None),
        P(None, "gz", "xy", None),
        P("gz", "xy", None),
        P(),
    )
    return jax.shard_map(
        shards,
        mesh=mesh,
        in_specs=placed,
        out_specs=(
            P(None, None, "gz", "xy", None),
            P(None, None, "gz", "xy", None),
            P(None, "gz", "xy", None),
        ),
        check_vma=False,
    )
```

profile of v0, /device:TPU:34, one launch (start us, length us, event | category | flops | bytes accessed | tf_op | source)
XLA Modules:
  0.0 287.0 jit_solution(10090494434730670370)
XLA Ops:
  0.6 0.7 fusion.1226
  1.4 0.7 convert_bitcast_fusion.2
  2.1 0.9 fusion.1254
  2.9 0.8 fusion.1253
  3.8 7.2 %collective-permute-start.1 = (f32[8,32,1,1,128]{4,1,0,3,2:T(8,128)S(1)}, f32[8,32,1,1,128]{4,1,0,3,2:T(8,128)S(1)}, u32[]{:S(2)}, u32[]{:S(2)}) collective-permute-start(f32[8,32,1,1,128]{4,1,0,3,2:T(8,128)S(1)} %pad_maximum_fusion.4), channel_id=1, source_target_pairs={{8,0},{16,8},{24,16},{32,24},{40,32},{48,40},{56,48},{64,56},{72,6... | collective-permute-start | bytes 393224 | tf_op jit(solution)/shard_map/ppermute | solution.py:28
  11.0 1.9 collective-permute-start
  13.5 7.7 %collective-permute-done = f32[8,32,1,1,128]{4,1,0,3,2:T(8,128)S(1)} collective-permute-done((f32[8,32,1,1,128]{4,1,0,3,2:T(8,128)S(1)}, f32[8,32,1,1,128]{4,1,0,3,2:T(8,128)S(1)}, u32[]{:S(2)}, u32[]{:S(2)}) %collective-permute-start) | collective-permute-done | bytes 131104 | tf_op jit(solution)/shard_map/ppermute | solution.py:25
  21.2 8.3 %collective-permute-start.3 = (f32[8,32,1,3,128]{4,1,0,3,2:T(8,128)S(1)}, f32[8,32,1,3,128]{4,1,0,3,2:T(8,128)S(1)}, u32[]{:S(2)}, u32[]{:S(2)}) collective-permute-start(f32[8,32,1,3,128]{4,1,0,3,2:T(8,128)S(1)} %pad_maximum_fusion.2), channel_id=1, source_target_pairs={{1,0},{2,1},{3,2},{4,3},{5,4},{6,5},{7,6},{0,7},{9,8},{10,9},{11,1... | collective-permute-start | bytes 1179656 | tf_op jit(solution)/shard_map/ppermute | solution.py:28
  29.5 1.9 collective-permute-start.2
  31.5 1.3 fusion.1267
  35.5 11.9 %collective-permute-done.3 = f32[8,32,1,3,128]{4,1,0,3,2:T(8,128)S(1)} collective-permute-done((f32[8,32,1,3,128]{4,1,0,3,2:T(8,128)S(1)}, f32[8,32,1,3,128]{4,1,0,3,2:T(8,128)S(1)}, u32[]{:S(2)}, u32[]{:S(2)}) %collective-permute-start.3) | collective-permute-done | bytes 393248 | tf_op jit(solution)/shard_map/ppermute | solution.py:28
  47.4 10.8 %collective-permute-done.2 = f32[8,32,1,3,128]{4,1,0,3,2:T(8,128)S(1)} collective-permute-done((f32[8,32,1,3,128]{4,1,0,3,2:T(8,128)S(1)}, f32[8,32,1,3,128]{4,1,0,3,2:T(8,128)S(1)}, u32[]{:S(2)}, u32[]{:S(2)}) %collective-permute-start.2) | collective-permute-done | bytes 393248 | tf_op jit(solution)/shard_map/ppermute | solution.py:25
  63.4 3.6 %multiply_reduce_fusion.63 = (f32[32,32,128]{2,1,0:T(8,128)S(1)}, f32[32,32,128]{2,1,0:T(8,128)S(1)}, f32[32,32,128]{2,1,0:T(8,128)S(1)}, f32[32,32,128]{2,1,0:T...) fusion(f32[3]{0:T(128)S(1)} %copy-done.116, ...), kind=kLoop, calls=%fused_computation.129 | loop fusion | flops 14942208 | bytes 6979644 | tf_op jit(solution)/shard_map/while/body/eval_jaxpr/reduce_sum | solution.py:38
  67.1 3.4 %multiply_reduce_fusion.57 = (f32[32,32,128]{2,1,0:T(8,128)S(1)}, f32[32,32,128]{2,1,0:T(8,128)S(1)}, f32[32,32,128]{2,1,0:T(8,128)S(1)}, f32[32,32,128]{2,1,0:T...) fusion(f32[3]{0:T(128)S(1)} %copy-done.117, ...), kind=kLoop, calls=%fused_computation.121 | loop fusion | flops 14942208 | bytes 6979644 | tf_op jit(solution)/shard_map/while/body/eval_jaxpr/reduce_sum | solution.py:38
  70.6 3.2 %fusion.340 = (f32[32,32,128]{2,1,0:T(8,128)S(1)}, f32[32,32,128]{2,1,0:T(8,128)S(1)}, f32[32,32,128]{2,1,0:T(8,128)S(1)}, f32[32,32,128]{2,1,0:T(8,128)S(1)}) fusion(f32[32,32,128]{2,1,0:T(8,128)S(1)} %get-tuple-element.525, f32[32,32,128]{2,1,0:T(8,128)S(1)} %get-tuple-element.526, s32[32,128]{1,0:T(8,128)S(1)} %get-tuple-element.927, ...), kind=kLoop, calls=%fused_computation.755 | loop fusion | flops 15728640 | bytes 6455296 | tf_op jit(solution)/shard_map/while/body/eval_jaxpr/div | solution.py:52
  73.9 3.2 %fusion.360 = (f32[32,32,128]{2,1,0:T(8,128)S(1)}, f32[32,32,128]{2,1,0:T(8,128)S(1)}, f32[32,32,128]{2,1,0:T(8,128)S(1)}, f32[32,32,128]{2,1,0:T(8,128)S(1)}) fusion(f32[32,32,128]{2,1,0:T(8,128)S(1)} %get-tuple-element.529, f32[32,32,128]{2,1,0:T(8,128)S(1)} %get-tuple-element.530, s32[32,128]{1,0:T(8,128)S(1)} %get-tuple-element.931, ...), kind=kLoop, calls=%fused_computation.775 | loop fusion | flops 15728640 | bytes 6455296 | tf_op jit(solution)/shard_map/while/body/eval_jaxpr/div | solution.py:52
  77.3 3.6 %multiply_reduce_fusion.66 = (f32[32,32,128]{2,1,0:T(8,128)S(1)}, f32[32,32,128]{2,1,0:T(8,128)S(1)}, f32[32,32,128]{2,1,0:T(8,128)S(1)}, f32[32,32,128]{2,1,0:T...) fusion(f32[3]{0:T(128)S(1)} %copy-done.110, ...), kind=kLoop, calls=%fused_computation.133 | loop fusion | flops 14012416 | bytes 6455356 | tf_op jit(solution)/shard_map/while/body/eval_jaxpr/reduce_sum | solution.py:38
  80.9 3.5 %multiply_reduce_fusion.60 = (f32[32,32,128]{2,1,0:T(8,128)S(1)}, f32[32,32,128]{2,1,0:T(8,128)S(1)}, f32[32,32,128]{2,1,0:T(8,128)S(1)}, f32[32,32,128]{2,1,0:T...) fusion(f32[3]{0:T(128)S(1)} %copy-done.119, ...), kind=kLoop, calls=%fused_computation.125 | loop fusion | flops 14548992 | bytes 6979644 | tf_op jit(solution)/shard_map/while/body/eval_jaxpr/reduce_sum | solution.py:38
  84.4 3.4 %fusion.400 = (f32[32,32,128]{2,1,0:T(8,128)S(1)}, f32[32,32,128]{2,1,0:T(8,128)S(1)}, f32[32,32,128]{2,1,0:T(8,128)S(1)}, f32[32,32,128]{2,1,0:T(8,128)S(1)}) fusion(f32[32,32,128]{2,1,0:T(8,128)S(1)} %get-tuple-element.537, f32[32,32,128]{2,1,0:T(8,128)S(1)} %get-tuple-element.538, s32[32,128]{1,0:T(8,128)S(1)} %get-tuple-element.937, ...), kind=kLoop, calls=%fused_computation.815 | loop fusion | flops 15859712 | bytes 6459392 | tf_op jit(solution)/shard_map/while/body/eval_jaxpr/div | solution.py:52
  87.9 3.3 %multiply_reduce_fusion.124 = (f32[3,32,128]{2,1,0:T(8,128)S(1)}, f32[3,32,128]{2,1,0:T(8,128)S(1)}, f32[32,32,128]{2,1,0:T(8,128)S(1)}, f32[32,32,128]{2,1,0:T(...) fusion(f32[3]{0:T(128)S(1)} %copy-done.107, ...), kind=kLoop, calls=%fused_computation.211 | loop fusion | flops 12689408 | bytes 5931068 | tf_op jit(solution)/shard_map/while/body/eval_jaxpr/reduce_sum | solution.py:58
  91.2 3.2 %fusion.320 = (f32[32,32,128]{2,1,0:T(8,128)S(1)}, f32[32,32,128]{2,1,0:T(8,128)S(1)}, f32[32,32,128]{2,1,0:T(8,128)S(1)}, f32[32,32,128]{2,1,0:T(8,128)S(1)}) fusion(f32[32,32,128]{2,1,0:T(8,128)S(1)} %get-tuple-element.519, f32[32,32,128]{2,1,0:T(8,128)S(1)} %get-tuple-element.520, s32[32,128]{1,0:T(8,128)S(1)} %get-tuple-element.779, ...), kind=kLoop, calls=%fused_computation.735 | loop fusion | flops 15728640 | bytes 6455296 | tf_op jit(solution)/shard_map/while/body/eval_jaxpr/div | solution.py:52
  94.5 3.2 %fusion.300 = (f32[32,32,128]{2,1,0:T(8,128)S(1)}, f32[32,32,128]{2,1,0:T(8,128)S(1)}, f32[32,32,128]{2,1,0:T(8,128)S(1)}, f32[32,32,128]{2,1,0:T(8,128)S(1)}) fusion(f32[32,32,128]{2,1,0:T(8,128)S(1)} %get-tuple-element.515, f32[32,32,128]{2,1,0:T(8,128)S(1)} %get-tuple-element.516, s32[32,128]{1,0:T(8,128)S(1)} %get-tuple-element.929, ...), kind=kLoop, calls=%fused_computation.715 | loop fusion | flops 15728640 | bytes 6455296 | tf_op jit(solution)/shard_map/while/body/eval_jaxpr/div | solution.py:52
  97.7 3.2 %fusion.310 = (f32[32,32,128]{2,1,0:T(8,128)S(1)}, f32[32,32,128]{2,1,0:T(8,128)S(1)}, f32[32,32,128]{2,1,0:T(8,128)S(1)}, f32[32,32,128]{2,1,0:T(8,128)S(1)}) fusion(f32[32,32,128]{2,1,0:T(8,128)S(1)} %get-tuple-element.517, f32[32,32,128]{2,1,0:T(8,128)S(1)} %get-tuple-element.518, s32[32,128]{1,0:T(8,128)S(1)} %get-tuple-element.1112, ...), kind=kLoop, calls=%fused_computation.725 | loop fusion | flops 15728640 | bytes 6455296 | tf_op jit(solution)/shard_map/while/body/eval_jaxpr/div | solution.py:52
  100.9 2.3 multiply_reduce_fusion.115
  103.2 2.3 multiply_reduce_fusion.112
  105.6 2.8 fusion.440
  108.4 2.4 multiply_reduce_fusion.121
  110.8 2.3 multiply_reduce_fusion.118
  113.3 4.7 %collective-permute-start.5 = (f32[8,32,1,1,128]{4,1,0,2,3:T(8,128)S(1)}, f32[8,32,1,1,128]{4,1,0,2,3:T(8,128)S(1)}, u32[]{:S(2)}, u32[]{:S(2)}) collective-permute-start(f32[8,32,1,1,128]{4,1,0,2,3:T(8,128)S(1)} %pad_maximum_fusion.5), channel_id=1, source_target_pairs={{8,0},{16,8},{24,16},{32,24},{40,32},{48,40},{56,48},{64,56},{72,6... | collective-permute-start | bytes 393224 | tf_op jit(solution)/shard_map/ppermute | solution.py:28
  117.9 1.9 collective-permute-start.4
  120.4 7.7 %collective-permute-done.4 = f32[8,32,1,1,128]{4,1,0,2,3:T(8,128)S(1)} collective-permute-done((f32[8,32,1,1,128]{4,1,0,2,3:T(8,128)S(1)}, f32[8,32,1,1,128]{4,1,0,2,3:T(8,128)S(1)}, u32[]{:S(2)}, u32[]{:S(2)}) %collective-permute-start.4) | collective-permute-done | bytes 131104 | tf_op jit(solution)/shard_map/ppermute | solution.py:25
  128.2 8.0 %collective-permute-start.7 = (f32[8,32,1,3,128]{4,1,0,2,3:T(8,128)S(1)}, f32[8,32,1,3,128]{4,1,0,2,3:T(8,128)S(1)}, u32[]{:S(2)}, u32[]{:S(2)}) collective-permute-start(f32[8,32,1,3,128]{4,1,0,2,3:T(8,128)S(1)} %pad_maximum_fusion.3), channel_id=1, source_target_pairs={{1,0},{2,1},{3,2},{4,3},{5,4},{6,5},{7,6},{0,7},{9,8},{10,9},{11,1... | collective-permute-start | bytes 1179656 | tf_op jit(solution)/shard_map/ppermute | solution.py:28
  136.2 1.9 collective-permute-start.6
  140.8 21.0 %collective-permute-done.7 = f32[8,32,1,3,128]{4,1,0,2,3:T(8,128)S(1)} collective-permute-done((f32[8,32,1,3,128]{4,1,0,2,3:T(8,128)S(1)}, f32[8,32,1,3,128]{4,1,0,2,3:T(8,128)S(1)}, u32[]{:S(2)}, u32[]{:S(2)}) %collective-permute-start.7) | collective-permute-done | bytes 393248 | tf_op jit(solution)/shard_map/ppermute | solution.py:28
  161.7 7.5 %collective-permute-done.6 = f32[8,32,1,3,128]{4,1,0,2,3:T(8,128)S(1)} collective-permute-done((f32[8,32,1,3,128]{4,1,0,2,3:T(8,128)S(1)}, f32[8,32,1,3,128]{4,1,0,2,3:T(8,128)S(1)}, u32[]{:S(2)}, u32[]{:S(2)}) %collective-permute-start.6) | collective-permute-done | bytes 393248 | tf_op jit(solution)/shard_map/ppermute | solution.py:25
  182.3 0.7 fusion.945
  183.6 0.7 fusion.949
  188.2 3.6 %multiply_reduce_fusion.7 = (f32[32,32,128]{2,1,0:T(8,128)S(1)}, f32[32,32,128]{2,1,0:T(8,128)S(1)}, f32[32,32,128]{2,1,0:T(8,128)S(1)}, f32[32,32,128]{2,1,0:T(...) fusion(f32[3]{0:T(128)S(1)} %copy-done.116, ...), kind=kLoop, calls=%fused_computation.24 | loop fusion | flops 14942208 | bytes 6979644 | tf_op jit(solution)/shard_map/while/body/eval_jaxpr/reduce_sum | solution.py:38
  192.0 3.4 %multiply_reduce_fusion.5 = (f32[32,32,128]{2,1,0:T(8,128)S(1)}, f32[32,32,128]{2,1,0:T(8,128)S(1)}, f32[32,32,128]{2,1,0:T(8,128)S(1)}, f32[32,32,128]{2,1,0:T(...) fusion(f32[3]{0:T(128)S(1)} %copy-done.120, ...), kind=kLoop, calls=%fused_computation.20 | loop fusion | flops 14548992 | bytes 6979644 | tf_op jit(solution)/shard_map/while/body/eval_jaxpr/reduce_sum | solution.py:38
  195.6 3.5 %multiply_reduce_fusion.3 = (f32[32,32,128]{2,1,0:T(8,128)S(1)}, f32[32,32,128]{2,1,0:T(8,128)S(1)}, f32[32,32,128]{2,1,0:T(8,128)S(1)}, f32[32,32,128]{2,1,0:T(...) fusion(f32[3]{0:T(128)S(1)} %copy-done.118, ...), kind=kLoop, calls=%fused_computation.16 | loop fusion | flops 14942208 | bytes 6979644 | tf_op jit(solution)/shard_map/while/body/eval_jaxpr/reduce_sum | solution.py:38
  199.0 2.4 fusion.760
  201.5 4.1 %fusion.560 = (f32[32,32,128]{2,1,0:T(8,128)}, f32[32,32,128]{2,1,0:T(8,128)S(1)}, f32[32,32,128]{2,1,0:T(8,128)}, f32[32,32,128]{2,1,0:T(8,128)S(1)}) fusion(f32[32,32,128]{2,1,0:T(8,128)S(1)} %get-tuple-element.557, f32[32,32,128]{2,1,0:T(8,128)S(1)} %get-tuple-element.558, s32[32,128]{1,0:T(8,128)S(1)} %get-tuple-element.709, ...), kind=kLoop, calls=%fused_computation.975 | loop fusion | flops 15859712 | bytes 6459392 | tf_op jit(solution)/shard_map/while/body/eval_jaxpr/div | solution.py:52
  205.7 4.2 %fusion.917 = (f32[3,32,128]{2,1,0:T(8,128)}, f32[3,32,128]{2,1,0:T(8,128)}, f32[32,32,128]{2,1,0:T(8,128)S(1)}, f32[32,32,128]{2,1,0:T(8,128)S(1)}, f32[32,32,1...) fusion(f32[3,32,128]{2,1,0:T(8,128)S(1)} %get-tuple-element.739, ...), kind=kLoop, calls=%fused_computation.1886 | loop fusion | flops 12689408 | bytes 18513968 | tf_op jit(solution)/shard_map/while/body/eval_jaxpr/reduce_sum | solution.py:58
  209.9 1.0 multiply_reduce_fusion.182
  211.5 1.0 multiply_reduce_fusion.130
  213.1 2.1 multiply_reduce_fusion.9
  215.4 3.2 %fusion.680 = (f32[32,32,128]{2,1,0:T(8,128)S(1)}, f32[32,32,128]{2,1,0:T(8,128)S(1)}, f32[32,32,128]{2,1,0:T(8,128)S(1)}, f32[32,32,128]{2,1,0:T(8,128)S(1)}) fusion(f32[32,32,128]{2,1,0:T(8,128)S(1)} %get-tuple-element.583, f32[32,32,128]{2,1,0:T(8,128)S(1)} %get-tuple-element.584, s32[32,128]{1,0:T(8,128)S(1)} %copy-done.64, ...), kind=kLoop, calls=%fused_computation.1095 | loop fusion | flops 15728640 | bytes 6455296 | tf_op jit(solution)/shard_map/while/body/eval_jaxpr/div | solution.py:52
  218.6 1.1 fusion.11
  219.8 1.0 multiply_reduce_fusion.154
  221.4 3.9 %fusion.540 = (f32[32,32,128]{2,1,0:T(8,128)}, f32[32,32,128]{2,1,0:T(8,128)S(1)}, f32[32,32,128]{2,1,0:T(8,128)S(1)}, f32[32,32,128]{2,1,0:T(8,128)S(1)}) fusion(f32[32,32,128]{2,1,0:T(8,128)S(1)} %get-tuple-element.553, f32[32,32,128]{2,1,0:T(8,128)S(1)} %get-tuple-element.554, s32[32,128]{1,0:T(8,128)S(1)} %copy-done.67, f32[32,128]{1,0:T(8,128)S(1)} %copy-done.66, ...), kind=kLoop, calls=%fused_computation.955 | loop fusion | flops 15728640 | bytes 6455296 | tf_op jit(solution)/shard_map/while/body/eval_jaxpr/div | solution.py:52
  225.5 3.9 %fusion.550 = (f32[32,32,128]{2,1,0:T(8,128)}, f32[32,32,128]{2,1,0:T(8,128)S(1)}, f32[32,32,128]{2,1,0:T(8,128)S(1)}, f32[32,32,128]{2,1,0:T(8,128)S(1)}) fusion(f32[32,32,128]{2,1,0:T(8,128)S(1)} %get-tuple-element.555, f32[32,32,128]{2,1,0:T(8,128)S(1)} %get-tuple-element.556, s32[32,128]{1,0:T(8,128)S(1)} %copy-done.61, f32[32,128]{1,0:T(8,128)S(1)} %copy-done.60, ...), kind=kLoop, calls=%fused_computation.965 | loop fusion | flops 15728640 | bytes 6455296 | tf_op jit(solution)/shard_map/while/body/eval_jaxpr/div | solution.py:52
  229.5 4.0 %fusion.580 = (f32[32,32,128]{2,1,0:T(8,128)}, f32[32,32,128]{2,1,0:T(8,128)S(1)}, f32[32,32,128]{2,1,0:T(8,128)S(1)}, f32[32,32,128]{2,1,0:T(8,128)}) fusion(f32[32,32,128]{2,1,0:T(8,128)S(1)} %get-tuple-element.561, f32[32,32,128]{2,1,0:T(8,128)S(1)} %get-tuple-element.562, s32[32,128]{1,0:T(8,128)S(1)} %copy-done.57, f32[32,128]{1,0:T(8,128)S(1)} %copy-done.56, ...), kind=kLoop, calls=%fused_computation.995 | loop fusion | flops 15728640 | bytes 6455296 | tf_op jit(solution)/shard_map/while/body/eval_jaxpr/div | solution.py:52
  233.6 5.8 %fusion.1245 = (f32[3,32,128]{2,1,0:T(8,128)}, f32[3,32,128]{2,1,0:T(8,128)}, f32[3,32,128]{2,1,0:T(8,128)}, f32[3,32,128]{2,1,0:T(8,128)}, f32[3,32,128]{2,1,0:...) fusion(f32[3]{0:T(128)S(1)} %copy-done.103, ...), kind=kLoop, calls=%fused_computation.2354 | loop fusion | flops 9363456 | bytes 19513416 | tf_op jit(solution)/shard_map/while/body/eval_jaxpr/reduce_sum | solution.py:58
  239.3 1.0 multiply_reduce_fusion.158
  240.9 1.0 multiply_reduce_fusion.150
  242.4 1.0 multiply_reduce_fusion.142
  243.4 1.0 multiply_reduce_fusion.134
  244.4 1.0 multiply_reduce_fusion.138
  245.3 1.0 multiply_reduce_fusion.146
  246.4 3.2 %fusion.600 = (f32[32,32,128]{2,1,0:T(8,128)S(1)}, f32[32,32,128]{2,1,0:T(8,128)S(1)}, f32[32,32,128]{2,1,0:T(8,128)S(1)}, f32[32,32,128]{2,1,0:T(8,128)S(1)}) fusion(f32[32,32,128]{2,1,0:T(8,128)S(1)} %get-tuple-element.565, f32[32,32,128]{2,1,0:T(8,128)S(1)} %get-tuple-element.566, s32[32,128]{1,0:T(8,128)S(1)} %get-tuple-element.859, ...), kind=kLoop, calls=%fused_computation.1015 | loop fusion | flops 15728640 | bytes 6455296 | tf_op jit(solution)/shard_map/while/body/eval_jaxpr/div | solution.py:52
  249.7 3.8 %fusion.1228 = (f32[3,32,128]{2,1,0:T(8,128)S(1)}, f32[3,32,128]{2,1,0:T(8,128)S(1)}, f32[3,32,128]{2,1,0:T(8,128)S(1)}, f32[3,32,128]{2,1,0:T(8,128)S(1)}, f32[...) fusion(f32[3]{0:T(128)S(1)} %copy-done.109, ...), kind=kLoop, calls=%fused_computation.2337 | loop fusion | flops 9363456 | bytes 21086280 | tf_op jit(solution)/shard_map/while/body/eval_jaxpr/reduce_sum | solution.py:58
  257.5 4.3 %fusion.1229 = (f32[3,32,128]{2,1,0:T(8,128)S(1)}, f32[3,32,128]{2,1,0:T(8,128)S(1)}, f32[3,32,128]{2,1,0:T(8,128)S(1)}, f32[3,32,128]{2,1,0:T(8,128)S(1)}, f32[...) fusion(f32[3]{0:T(128)S(1)} %copy-done.115, ...), kind=kLoop, calls=%fused_computation.2338 | loop fusion | flops 9363456 | bytes 22659144 | tf_op jit(solution)/shard_map/while/body/eval_jaxpr/reduce_sum | solution.py:58
  264.7 4.0 %fusion.915 = (f32[3,32,128]{2,1,0:T(8,128)S(1)}, f32[3,32,128]{2,1,0:T(8,128)S(1)}, f32[3,32,128]{2,1,0:T(8,128)S(1)}, f32[3,32,128]{2,1,0:T(8,128)S(1)}, f32[3...) fusion(f32[3,32,128]{2,1,0:T(8,128)S(1)} %copy-done.19, ...), kind=kLoop, calls=%fused_computation.1884 | loop fusion | flops 9363456 | bytes 22659132 | tf_op jit(solution)/shard_map/while/body/eval_jaxpr/reduce_sum | solution.py:58
  285.4 0.8 add_multiply_fusion
  (646 shorter events, 49.4 us)
Async XLA Ops:
  0.6 34.8 %copy-start.153 = (s32[1,1,128]{2,1,0:T(1,128)S(1)}, s32[1,1,128]{2,1,0:T(1,128)}, u32[]{:S(2)}) copy-start(s32[1,1,128]{2,1,0:T(1,128)} %param.76) | copy-start | bytes 1540
  3.8 9.7 %collective-permute-start.1 = (f32[8,32,1,1,128]{4,1,0,3,2:T(8,128)S(1)}, f32[8,32,1,1,128]{4,1,0,3,2:T(8,128)S(1)}, u32[]{:S(2)}, u32[]{:S(2)}) collective-permute-start(f32[8,32,1,1,128]{4,1,0,3,2:T(8,128)S(1)} %pad_maximum_fusion.4), channel_id=1, source_target_pairs={{8,0},{16,8},{24,16},{32,24},{40,32},{48,40},{56,48},{64,56},{72,6... | collective-permute-start | bytes 393224 | tf_op jit(solution)/shard_map/ppermute | solution.py:28
  11.0 10.2 %collective-permute-start = (f32[8,32,1,1,128]{4,1,0,3,2:T(8,128)S(1)}, f32[8,32,1,1,128]{4,1,0,3,2:T(8,128)S(1)}, u32[]{:S(2)}, u32[]{:S(2)}) collective-permute-start(f32[8,32,1,1,128]{4,1,0,3,2:T(8,128)S(1)} %pad_maximum_fusion.4), channel_id=1, source_target_pairs={{0,8},{8,16},{16,24},{24,32},{32,40},{40,48},{48,56},{56,64},{64,7... | collective-permute-start | bytes 393224 | tf_op jit(solution)/shard_map/ppermute | solution.py:25
  21.2 26.1 %collective-permute-start.3 = (f32[8,32,1,3,128]{4,1,0,3,2:T(8,128)S(1)}, f32[8,32,1,3,128]{4,1,0,3,2:T(8,128)S(1)}, u32[]{:S(2)}, u32[]{:S(2)}) collective-permute-start(f32[8,32,1,3,128]{4,1,0,3,2:T(8,128)S(1)} %pad_maximum_fusion.2), channel_id=1, source_target_pairs={{1,0},{2,1},{3,2},{4,3},{5,4},{6,5},{7,6},{0,7},{9,8},{10,9},{11,1... | collective-permute-start | bytes 1179656 | tf_op jit(solution)/shard_map/ppermute | solution.py:28
  29.5 28.6 %collective-permute-start.2 = (f32[8,32,1,3,128]{4,1,0,3,2:T(8,128)S(1)}, f32[8,32,1,3,128]{4,1,0,3,2:T(8,128)S(1)}, u32[]{:S(2)}, u32[]{:S(2)}) collective-permute-start(f32[8,32,1,3,128]{4,1,0,3,2:T(8,128)S(1)} %pad_maximum_fusion.2), channel_id=1, source_target_pairs={{0,1},{1,2},{2,3},{3,4},{4,5},{5,6},{6,7},{7,0},{8,9},{9,10},{10,1... | collective-permute-start | bytes 1179656 | tf_op jit(solution)/shard_map/ppermute | solution.py:25
  35.5 22.9 %copy-start.152 = (f32[8]{0:T(128)S(1)}, f32[8]{0:T(128)}, u32[]{:S(2)}) copy-start(f32[8]{0:T(128)} %constant.829) | copy-start | bytes 100
  113.3 7.2 %collective-permute-start.5 = (f32[8,32,1,1,128]{4,1,0,2,3:T(8,128)S(1)}, f32[8,32,1,1,128]{4,1,0,2,3:T(8,128)S(1)}, u32[]{:S(2)}, u32[]{:S(2)}) collective-permute-start(f32[8,32,1,1,128]{4,1,0,2,3:T(8,128)S(1)} %pad_maximum_fusion.5), channel_id=1, source_target_pairs={{8,0},{16,8},{24,16},{32,24},{40,32},{48,40},{56,48},{64,56},{72,6... | collective-permute-start | bytes 393224 | tf_op jit(solution)/shard_map/ppermute | solution.py:28
  117.9 10.2 %collective-permute-start.4 = (f32[8,32,1,1,128]{4,1,0,2,3:T(8,128)S(1)}, f32[8,32,1,1,128]{4,1,0,2,3:T(8,128)S(1)}, u32[]{:S(2)}, u32[]{:S(2)}) collective-permute-start(f32[8,32,1,1,128]{4,1,0,2,3:T(8,128)S(1)} %pad_maximum_fusion.5), channel_id=1, source_target_pairs={{0,8},{8,16},{16,24},{24,32},{32,40},{40,48},{48,56},{56,64},{64,7... | collective-permute-start | bytes 393224 | tf_op jit(solution)/shard_map/ppermute | solution.py:25
  128.2 33.6 %collective-permute-start.7 = (f32[8,32,1,3,128]{4,1,0,2,3:T(8,128)S(1)}, f32[8,32,1,3,128]{4,1,0,2,3:T(8,128)S(1)}, u32[]{:S(2)}, u32[]{:S(2)}) collective-permute-start(f32[8,32,1,3,128]{4,1,0,2,3:T(8,128)S(1)} %pad_maximum_fusion.3), channel_id=1, source_target_pairs={{1,0},{2,1},{3,2},{4,3},{5,4},{6,5},{7,6},{0,7},{9,8},{10,9},{11,1... | collective-permute-start | bytes 1179656 | tf_op jit(solution)/shard_map/ppermute | solution.py:28
  136.2 33.1 %collective-permute-start.6 = (f32[8,32,1,3,128]{4,1,0,2,3:T(8,128)S(1)}, f32[8,32,1,3,128]{4,1,0,2,3:T(8,128)S(1)}, u32[]{:S(2)}, u32[]{:S(2)}) collective-permute-start(f32[8,32,1,3,128]{4,1,0,2,3:T(8,128)S(1)} %pad_maximum_fusion.3), channel_id=1, source_target_pairs={{0,1},{1,2},{2,3},{3,4},{4,5},{5,6},{6,7},{7,0},{8,9},{9,10},{10,1... | collective-permute-start | bytes 1179656 | tf_op jit(solution)/shard_map/ppermute | solution.py:25
  170.8 21.0 %copy-start.9 = (f32[3,32,128]{2,1,0:T(8,128)}, f32[3,32,128]{2,1,0:T(8,128)S(1)}, u32[]{:S(2)}) copy-start(f32[3,32,128]{2,1,0:T(8,128)S(1)} %get-tuple-element.750) | copy-start | bytes 147460
  170.8 24.6 %copy-start.7 = (f32[3,32,128]{2,1,0:T(8,128)}, f32[3,32,128]{2,1,0:T(8,128)S(1)}, u32[]{:S(2)}) copy-start(f32[3,32,128]{2,1,0:T(8,128)S(1)} %get-tuple-element.748) | copy-start | bytes 147460
  172.1 23.3 %copy-start.11 = (f32[3,32,128]{2,1,0:T(8,128)}, f32[3,32,128]{2,1,0:T(8,128)S(1)}, u32[]{:S(2)}) copy-start(f32[3,32,128]{2,1,0:T(8,128)S(1)} %get-tuple-element.744) | copy-start | bytes 147460
  172.1 33.5 %copy-start.15 = (f32[3,32,128]{2,1,0:T(8,128)}, f32[3,32,128]{2,1,0:T(8,128)S(1)}, u32[]{:S(2)}) copy-start(f32[3,32,128]{2,1,0:T(8,128)S(1)} %get-tuple-element.747) | copy-start | bytes 147460
  174.6 20.9 %copy-start.20 = (f32[3,32,128]{2,1,0:T(8,128)}, f32[3,32,128]{2,1,0:T(8,128)S(1)}, u32[]{:S(2)}) copy-start(f32[3,32,128]{2,1,0:T(8,128)S(1)} %get-tuple-element.890) | copy-start | bytes 147460
  174.7 17.1 %copy-start.16 = (f32[3,32,128]{2,1,0:T(8,128)}, f32[3,32,128]{2,1,0:T(8,128)S(1)}, u32[]{:S(2)}) copy-start(f32[3,32,128]{2,1,0:T(8,128)S(1)} %get-tuple-element.914) | copy-start | bytes 147460
  175.5 16.3 %copy-start.22 = (f32[3,32,128]{2,1,0:T(8,128)}, f32[3,32,128]{2,1,0:T(8,128)S(1)}, u32[]{:S(2)}) copy-start(f32[3,32,128]{2,1,0:T(8,128)S(1)} %get-tuple-element.916) | copy-start | bytes 147460
  175.7 16.1 %copy-start.24 = (f32[3,32,128]{2,1,0:T(8,128)}, f32[3,32,128]{2,1,0:T(8,128)S(1)}, u32[]{:S(2)}) copy-start(f32[3,32,128]{2,1,0:T(8,128)S(1)} %get-tuple-element.918) | copy-start | bytes 147460
  176.5 18.9 %copy-start.26 = (f32[3,32,128]{2,1,0:T(8,128)}, f32[3,32,128]{2,1,0:T(8,128)S(1)}, u32[]{:S(2)}) copy-start(f32[3,32,128]{2,1,0:T(8,128)S(1)} %get-tuple-element.892) | copy-start | bytes 147460
  177.3 18.2 %copy-start.18 = (f32[3,32,128]{2,1,0:T(8,128)}, f32[3,32,128]{2,1,0:T(8,128)S(1)}, u32[]{:S(2)}) copy-start(f32[3,32,128]{2,1,0:T(8,128)S(1)} %get-tuple-element.894) | copy-start | bytes 147460
  178.5 27.1 %copy-start.34 = (f32[3,32,128]{2,1,0:T(8,128)}, f32[3,32,128]{2,1,0:T(8,128)S(1)}, u32[]{:S(2)}) copy-start(f32[3,32,128]{2,1,0:T(8,128)S(1)} %get-tuple-element.896) | copy-start | bytes 147460
  178.9 13.0 %copy-start.35 = (f32[3,32,128]{2,1,0:T(8,128)}, f32[3,32,128]{2,1,0:T(8,128)S(1)}, u32[]{:S(2)}) copy-start(f32[3,32,128]{2,1,0:T(8,128)S(1)} %get-tuple-element.921) | copy-start | bytes 147460
  179.6 12.1 %copy-start.36 = (f32[3,32,128]{2,1,0:T(8,128)}, f32[3,32,128]{2,1,0:T(8,128)S(1)}, u32[]{:S(2)}) copy-start(f32[3,32,128]{2,1,0:T(8,128)S(1)} %get-tuple-element.913) | copy-start | bytes 147460
  186.5 5.3 %copy-start.28 = (f32[3,32,128]{2,1,0:T(8,128)}, f32[3,32,128]{2,1,0:T(8,128)S(1)}, u32[]{:S(2)}) copy-start(f32[3,32,128]{2,1,0:T(8,128)S(1)} %get-tuple-element.906) | copy-start | bytes 147460
  187.3 4.5 %copy-start.30 = (f32[3,32,128]{2,1,0:T(8,128)}, f32[3,32,128]{2,1,0:T(8,128)S(1)}, u32[]{:S(2)}) copy-start(f32[3,32,128]{2,1,0:T(8,128)S(1)} %get-tuple-element.908) | copy-start | bytes 147460
  201.5 4.2 %copy-start.87 = (f32[3]{0:T(128)S(1)}, f32[3]{0:T(128)}, u32[]{:S(2)}) copy-start(f32[3]{0:T(128)} %constant.874) | copy-start | bytes 40
  201.5 4.2 %copy-start.99 = (f32[3]{0:T(128)S(1)}, f32[3]{0:T(128)}, u32[]{:S(2)}) copy-start(f32[3]{0:T(128)} %constant.877) | copy-start | bytes 40
  201.5 4.2 %copy-start.102 = (f32[3]{0:T(128)S(1)}, f32[3]{0:T(128)}, u32[]{:S(2)}) copy-start(f32[3]{0:T(128)} %constant.875) | copy-start | bytes 40
  201.5 4.2 %copy-start.105 = (f32[3]{0:T(128)S(1)}, f32[3]{0:T(128)}, u32[]{:S(2)}) copy-start(f32[3]{0:T(128)} %constant.876) | copy-start | bytes 40
  221.3 4.0 %copy-start.60 = (f32[32,128]{1,0:T(8,128)S(1)}, f32[32,128]{1,0:T(8,128)}, u32[]{:S(2)}) copy-start(f32[32,128]{1,0:T(8,128)} %get-tuple-element.850) | copy-start | bytes 49156
  221.3 4.0 %copy-start.61 = (s32[32,128]{1,0:T(8,128)S(1)}, s32[32,128]{1,0:T(8,128)}, u32[]{:S(2)}) copy-start(s32[32,128]{1,0:T(8,128)} %get-tuple-element.851) | copy-start | bytes 49156
  221.3 4.0 %copy-start.68 = (f32[32,128]{1,0:T(8,128)S(1)}, f32[32,128]{1,0:T(8,128)}, u32[]{:S(2)}) copy-start(f32[32,128]{1,0:T(8,128)} %get-tuple-element.878) | copy-start | bytes 49156
  221.4 4.0 %copy-start.69 = (s32[32,128]{1,0:T(8,128)S(1)}, s32[32,128]{1,0:T(8,128)}, u32[]{:S(2)}) copy-start(s32[32,128]{1,0:T(8,128)} %get-tuple-element.879) | copy-start | bytes 49156
  221.4 4.0 %copy-start.74 = (f32[32,128]{1,0:T(8,128)S(1)}, f32[32,128]{1,0:T(8,128)}, u32[]{:S(2)}) copy-start(f32[32,128]{1,0:T(8,128)} %get-tuple-element.872) | copy-start | bytes 49156
  221.4 4.0 %copy-start.75 = (s32[32,128]{1,0:T(8,128)S(1)}, s32[32,128]{1,0:T(8,128)}, u32[]{:S(2)}) copy-start(s32[32,128]{1,0:T(8,128)} %get-tuple-element.873) | copy-start | bytes 49156
  221.4 4.0 %copy-start.82 = (f32[32,128]{1,0:T(8,128)S(1)}, f32[32,128]{1,0:T(8,128)}, u32[]{:S(2)}) copy-start(f32[32,128]{1,0:T(8,128)} %get-tuple-element.860) | copy-start | bytes 49156
  221.4 4.0 %copy-start.83 = (s32[32,128]{1,0:T(8,128)S(1)}, s32[32,128]{1,0:T(8,128)}, u32[]{:S(2)}) copy-start(s32[32,128]{1,0:T(8,128)} %get-tuple-element.861) | copy-start | bytes 49156
  225.4 4.0 %copy-start.51 = (f32[32,128]{1,0:T(8,128)S(1)}, f32[32,128]{1,0:T(8,128)}, u32[]{:S(2)}) copy-start(f32[32,128]{1,0:T(8,128)} %get-tuple-element.708) | copy-start | bytes 49156
  229.4 4.1 %copy-start.12 = (f32[3,32,128]{2,1,0:T(8,128)S(1)}, f32[3,32,128]{2,1,0:T(8,128)}, u32[]{:S(2)}) copy-start(f32[3,32,128]{2,1,0:T(8,128)} %copy-done.11) | copy-start | bytes 147460
  229.5 4.1 %copy-start.14 = (f32[3,32,128]{2,1,0:T(8,128)S(1)}, f32[3,32,128]{2,1,0:T(8,128)}, u32[]{:S(2)}) copy-start(f32[3,32,128]{2,1,0:T(8,128)} %get-tuple-element.745) | copy-start | bytes 147460
  229.5 4.1 %copy-start.100 = (f32[3]{0:T(128)S(1)}, f32[3]{0:T(128)}, u32[]{:S(2)}) copy-start(f32[3]{0:T(128)} %constant.877) | copy-start | bytes 40
  229.5 4.1 %copy-start.103 = (f32[3]{0:T(128)S(1)}, f32[3]{0:T(128)}, u32[]{:S(2)}) copy-start(f32[3]{0:T(128)} %constant.875) | copy-start | bytes 40
  229.5 4.1 %copy-start.112 = (f32[3]{0:T(128)S(1)}, f32[3]{0:T(128)}, u32[]{:S(2)}) copy-start(f32[3]{0:T(128)} %constant.878) | copy-start | bytes 40
  270.9 4.2 %copy-start.150 = (f32[6,1,1,128]{3,2,1,0:T(1,128)S(1)}, f32[6,1,1,128]{3,2,1,0:T(1,128)}, u32[]{:S(2)}) copy-start(f32[6,1,1,128]{3,2,1,0:T(1,128)} %constant_dynamic-update-slice_fusion.131) | copy-start | bytes 9220
  270.9 12.5 %copy-start.180 = (f32[128]{0:T(128)S(1)}, f32[128]{0:T(128)}, u32[]{:S(2)}) copy-start(f32[128]{0:T(128)} %get-tuple-element.399) | copy-start | bytes 1540
  270.9 12.5 %copy-start.178 = (f32[128]{0:T(128)S(1)}, f32[128]{0:T(128)}, u32[]{:S(2)}) copy-start(f32[128]{0:T(128)} %get-tuple-element.397) | copy-start | bytes 1540
  271.0 13.1 %copy-start.179 = (f32[128]{0:T(128)S(1)}, f32[128]{0:T(128)}, u32[]{:S(2)}) copy-start(f32[128]{0:T(128)} %get-tuple-element.394) | copy-start | bytes 1540
  271.0 13.1 %copy-start.177 = (f32[128]{0:T(128)S(1)}, f32[128]{0:T(128)}, u32[]{:S(2)}) copy-start(f32[128]{0:T(128)} %get-tuple-element.392) | copy-start | bytes 1540
  271.0 13.1 %copy-start.175 = (f32[128]{0:T(128)S(1)}, f32[128]{0:T(128)}, u32[]{:S(2)}) copy-start(f32[128]{0:T(128)} %get-tuple-element.393) | copy-start | bytes 1540
  271.0 13.1 %copy-start.173 = (f32[128]{0:T(128)S(1)}, f32[128]{0:T(128)}, u32[]{:S(2)}) copy-start(f32[128]{0:T(128)} %get-tuple-element.391) | copy-start | bytes 1540
  271.0 13.1 %copy-start.176 = (f32[128]{0:T(128)S(1)}, f32[128]{0:T(128)}, u32[]{:S(2)}) copy-start(f32[128]{0:T(128)} %get-tuple-element.383) | copy-start | bytes 1540
  271.0 13.1 %copy-start.174 = (f32[128]{0:T(128)S(1)}, f32[128]{0:T(128)}, u32[]{:S(2)}) copy-start(f32[128]{0:T(128)} %get-tuple-element.382) | copy-start | bytes 1540
  271.0 13.1 %copy-start.172 = (f32[128]{0:T(128)S(1)}, f32[128]{0:T(128)}, u32[]{:S(2)}) copy-start(f32[128]{0:T(128)} %get-tuple-element.380) | copy-start | bytes 1540
  271.0 13.1 %copy-start.171 = (f32[128]{0:T(128)S(1)}, f32[128]{0:T(128)}, u32[]{:S(2)}) copy-start(f32[128]{0:T(128)} %get-tuple-element.381) | copy-start | bytes 1540
  271.0 13.2 %copy-start.170 = (f32[128]{0:T(128)S(1)}, f32[128]{0:T(128)}, u32[]{:S(2)}) copy-start(f32[128]{0:T(128)} %get-tuple-element.379) | copy-start | bytes 1540
  271.0 14.3 %copy-start.37 = (f32[3,32,128]{2,1,0:T(8,128)S(1)}, f32[3,32,128]{2,1,0:T(8,128)}, u32[]{:S(2)}) copy-start(f32[3,32,128]{2,1,0:T(8,128)} %get-tuple-element.611) | copy-start | bytes 147460
  271.1 14.3 %copy-start.38 = (f32[3,32,128]{2,1,0:T(8,128)S(1)}, f32[3,32,128]{2,1,0:T(8,128)}, u32[]{:S(2)}) copy-start(f32[3,32,128]{2,1,0:T(8,128)} %get-tuple-element.612) | copy-start | bytes 147460
  271.1 14.3 %copy-start.44 = (f32[3,32,128]{2,1,0:T(8,128)S(1)}, f32[3,32,128]{2,1,0:T(8,128)}, u32[]{:S(2)}) copy-start(f32[3,32,128]{2,1,0:T(8,128)} %get-tuple-element.702) | copy-start | bytes 147460
  271.1 14.3 %copy-start.45 = (f32[3,32,128]{2,1,0:T(8,128)S(1)}, f32[3,32,128]{2,1,0:T(8,128)}, u32[]{:S(2)}) copy-start(f32[3,32,128]{2,1,0:T(8,128)} %get-tuple-element.621) | copy-start | bytes 147460
  271.1 14.3 %copy-start.46 = (f32[3,32,128]{2,1,0:T(8,128)S(1)}, f32[3,32,128]{2,1,0:T(8,128)}, u32[]{:S(2)}) copy-start(f32[3,32,128]{2,1,0:T(8,128)} %get-tuple-element.622) | copy-start | bytes 147460
  271.1 14.3 %copy-start.47 = (f32[3,32,128]{2,1,0:T(8,128)S(1)}, f32[3,32,128]{2,1,0:T(8,128)}, u32[]{:S(2)}) copy-start(f32[3,32,128]{2,1,0:T(8,128)} %get-tuple-element.623) | copy-start | bytes 147460
  271.1 14.3 %copy-start.48 = (f32[3,32,128]{2,1,0:T(8,128)S(1)}, f32[3,32,128]{2,1,0:T(8,128)}, u32[]{:S(2)}) copy-start(f32[3,32,128]{2,1,0:T(8,128)} %get-tuple-element.624) | copy-start | bytes 147460
  271.1 14.3 %copy-start.49 = (f32[3,32,128]{2,1,0:T(8,128)S(1)}, f32[3,32,128]{2,1,0:T(8,128)}, u32[]{:S(2)}) copy-start(f32[3,32,128]{2,1,0:T(8,128)} %get-tuple-element.625) | copy-start | bytes 147460
  271.1 14.3 %copy-start.50 = (f32[3,32,128]{2,1,0:T(8,128)S(1)}, f32[3,32,128]{2,1,0:T(8,128)}, u32[]{:S(2)}) copy-start(f32[3,32,128]{2,1,0:T(8,128)} %get-tuple-element.626) | copy-start | bytes 147460
  (125 other events, 254.6 us)
where the time goes:
time: 292 us; the launch traced here: 287 us
  other arithmetic  150 us (51%)
  waiting for transfers between devices  67.7 us (23%)
  starting transfers between devices  35.9 us (12%)
  local copies, waits for them, and re-layouts  23.7 us (8%)
  between operations  9.78 us (3%)
    div x14, other arithmetic, pair_terms(): (CONSERVATIVE * weight - FRICTION * weight * weight * approach + NOISE_LE...  47.3 us
    reduce_sum x10, other arithmetic, pair_terms(): home_force = jnp.sum(pair_force, axis=2)  34.6 us
    ppermute x4, waiting for transfers between devices, with_halo(): lax.ppermute(lax.slice_in_dim(block, 0, width, axis=dim), axis, backward)  34 us
    ppermute x4, waiting for transfers between devices, with_halo(): lax.ppermute(lax.slice_in_dim(block, block.shape[dim] - width, None, axis...  33.8 us
    ppermute x4, starting transfers between devices, with_halo(): lax.ppermute(lax.slice_in_dim(block, 0, width, axis=dim), axis, backward)  28.2 us
    reduce_sum x8, other arithmetic, pair_terms(): squared = jnp.sum(separation * separation, axis=0)  26.8 us
    unnamed x497, local copies, waits for them, and re-layouts  16.5 us
    reduce_sum x27, other arithmetic, pair_terms(): jnp.sum(separation[first] * pair_force[second], axis=(0, 1))  15.8 us
  transfers between devices with their start and end apart: 8, of which 8 were waited for; matrix products, arithmetic and copies ran while one was open for 0% of the time, Pallas kernels for 0%

commit v1 on v0

v1 whole, which is shorter than its diff:
```python
import functools
import math

import jax
import jax.numpy as jnp
from jax import lax
from jax.experimental import pallas as pl
from jax.experimental.pallas import tpu as pltpu
from jax.sharding import PartitionSpec as P

DT = 0.04
PRIME = 65521
FAR = 1048576.0
NOISE = 3.0 * math.sqrt(12.0) / math.sqrt(DT)
UNIT = NOISE / 2.0**32
BIAS = 32768
OFFSET = 25.0 / UNIT - BIAS
DRAG = 4.5 / UNIT
PAIRS = [(0, 0), (1, 1), (2, 2), (0, 1), (0, 2), (1, 2)]
LANES = 128
C = 4


def phase(x):
    rest = jnp.floor(x.astype(jnp.float32) * (225.0 / PRIME) + 0.5).astype(jnp.int32)
    return x * jnp.int32(65551) + rest


def roll(x, shift):
    return pltpu.roll(x, shift, axis=x.ndim - 1)


def kernel(
    ny, nz, pos, vel, frc, seeds, counts, offsets, f_out, v_out, s_out,
    snd0, snd1, yp0, yp1, ym0, ym1, zp0, zp1, ry0, ry1, rz0, rz1, vz,
    rfm0, rfm1, rfp0, rfp1, rzm0, rzm1, vzm,
    ig, ii, jof, joi, jzf, jzi, gpart, facc, jacc_o, jacc_z, vi, vj_o, vj_z, send, recv,
):
    iy = lax.axis_index("xy")
    iz = lax.axis_index("gz")
    up_y = {"xy": lax.rem(iy + 1, ny), "gz": iz}
    dn_y = {"xy": lax.rem(iy + ny - 1, ny), "gz": iz}
    up_z = {"xy": iy, "gz": lax.rem(iz + 1, nz)}
    dn_z = {"xy": iy, "gz": lax.rem(iz + nz - 1, nz)}
    barrier = pltpu.get_barrier_semaphore()
    for where in (up_y, dn_y, up_z, dn_z):
        pl.semaphore_signal(barrier, inc=1, device_id=where, device_id_type=pl.DeviceIdType.MESH)

    started = []

    def remote(src, dst, step, slot, where):
        copy = pltpu.make_async_remote_copy(
            src_ref=src, dst_ref=dst, send_sem=send.at[step, slot], recv_sem=recv.at[step, slot],
            device_id=where, device_id_type=pl.DeviceIdType.MESH,
        )
        started.append(copy)
        return copy

    slot_no = (
        lax.broadcasted_iota(jnp.int32, (C, 8, LANES), 0) * 8 + lax.broadcasted_iota(jnp.int32, (C, 8, LANES), 1)
    )
    present = slot_no < counts[...]

    def tile(g, jf, ji, dxi, c, react, at):
        force = [[jnp.zeros((8, LANES), jnp.float32) for _ in range(4)] for _ in range(3)]
        for j in range(8):
            near = [jnp.broadcast_to(jf[dxi, c, k, j : j + 1, :], (8, LANES)) for k in range(6)]
            seed_j = jnp.broadcast_to(ji[dxi, c, 0, j : j + 1, :], (8, LANES))
            base_j = jnp.broadcast_to(ji[dxi, c, 1, j : j + 1, :], (8, LANES))
            back = [None, None, None]
            for a in range(4):
                d = [ig[g, k, a] - near[k] for k in range(3)]
                u = [ig[g, 3 + k, a] - near[3 + k] for k in range(3)]
                square = d[0] * d[0] + d[1] * d[1] + d[2] * d[2]
                inverse = lax.rsqrt(jnp.maximum(square, 0.0025))
                gap = jnp.maximum(inverse - 1.0, 0.0)
                drag = d[0] * u[0] + d[1] * u[1] + d[2] * u[2]
                angle = ii[g, 0, a] * seed_j + (ii[g, 1, a] + base_j)
                size = gap * ((angle.astype(jnp.float32) + OFFSET) - gap * drag)
                for k in range(3):
                    part = size * d[k]
                    force[k][a] = force[k][a] + part
                    if react:
                        back[k] = part if back[k] is None else back[k] + part
            if react:
                for k in range(3):
                    gpart[at, k, 8 * j : 8 * j + 8, :] = back[k]
        total = None
        if react:
            total = []
            for k in range(3):
                rows = [gpart[at, k, pl.ds(s, 8, stride=8), :] for s in range(8)]
                while len(rows) > 1:
                    rows = [rows[i] + rows[i + 1] for i in range(0, len(rows), 2)]
                total.append(rows[0])
        return force, total

    def pair_virial(g, jf, dxi, c, force, total):
        out = []
        for first, second in PAIRS:
            part = None
            for a in range(4):
                term = ig[g, first, a] * force[second][a]
                part = term if part is None else part + term
            if total is None:
                part = part + part
            else:
                part = part - jf[dxi, c, first] * total[second]
            out.append(part)
        return out

    def add_force(g, forces):
        for k in range(3):
            for a in range(4):
                value = facc[g, k, a]
                for force in forces:
                    value = value + force[k][a]
                facc[g, k, a] = value

    def add_rows(ref, at, values):
        for k, value in enumerate(values):
            ref[(*at, k)] = ref[(*at, k)] + value

    def i_prep(g, block, seed, shift_y, shear, step, turn):
        for k in range(3):
            value = turn(block(k))
            if k == 1 and shift_y != 0.0:
                value = value + shift_y
            for a in range(4):
                ig[g, k, a] = value[a]
            speed = turn(block(3 + k))
            if k == 0 and shear is not None:
                speed = speed + shear
            speed = speed * DRAG
            for a in range(4):
                ig[g, 3 + k, a] = speed[a]
        first = turn(seed).astype(jnp.int32) + (7919 * step + 1)
        many = phase(2 * first + 1)
        alone = phase(first * (first + 1)) + jnp.int32(BIAS - 2**31)
        for a in range(4):
            ii[g, 0, a] = many[a]
            ii[g, 1, a] = alone[a]

    def j_prep(jf, c, value_of, shift_z):
        for k in range(6):
            value = value_of(c, k)
            if k == 2 and shift_z != 0.0:
                value = value + shift_z
            if k >= 3:
                value = value * DRAG
            for dxi in range(3):
                dx = dxi - 1
                moved = value if dx == 0 else roll(value, (-dx) % LANES)
                if k == 0 and dx != 0:
                    moved = moved + 2.0 * dx
                jf[dxi, c, k] = moved

    def j_seed(ji, c, seed):
        number = seed.astype(jnp.int32)
        base = phase(number * number)
        for dxi in range(3):
            dx = dxi - 1
            ji[dxi, c, 0] = number if dx == 0 else roll(number, (-dx) % LANES)
            ji[dxi, c, 1] = base if dx == 0 else roll(base, (-dx) % LANES)

    def back_to_place(values, dxi):
        dx = dxi - 1
        return [v if dx == 0 else roll(v, dx % LANES) for v in values]

    for step in range(2):
        last = step == 1
        snd, yp, ym, zp = (snd1, yp1, ym1, zp1) if last else (snd0, yp0, ym0, zp0)
        ry, rz, rfm, rfp, rzm = (ry1, rz1, rfm1, rfp1, rzm1) if last else (ry0, rz0, rfm0, rfp0, rzm0)
        for k in range(3):
            if not last:
                half = vel[k] + 0.5 * DT * frc[k]
                place = jnp.where(present, pos[k] + DT * half, FAR)
            else:
                half = v_out[k] + DT * f_out[k]
                old = jnp.stack([snd0[c, k] for c in range(C)])
                place = jnp.where(present, old + DT * half, FAR)
            for c in range(C):
                snd[c, k] = place[c]
                snd[c, 3 + k] = half[c]
        if not last:
            number = seeds[...].astype(jnp.float32)
            for c in range(C):
                snd[c, 6] = number[c]

        def own(k):
            return jnp.stack([snd[c, k] for c in range(C)])

        seed_own = jnp.stack([snd0[c, 6] for c in range(C)])
        i_prep(0, own, seed_own, 0.0, None, step, lambda v: v)
        if not last:
            pl.semaphore_wait(barrier, 4)
        send_z = [remote(snd.at[c], zp.at[c], step, c, dn_z) for c in range(C)]
        send_up = remote(snd, ym, step, 4, up_y)
        send_dn = remote(snd, yp, step, 5, dn_y)
        send_z[0].start()
        send_dn.start()
        send_up.start()
        for c in range(1, C):
            send_z[c].start()

        for c in range(C):
            j_prep(jof, c, lambda c, k: snd[c, k], 0.0)
            if not last:
                j_seed(joi, c, snd0[c, 6])
        zero = jnp.zeros((8, LANES), jnp.float32)
        for g in range(3):
            for k in range(3):
                for a in range(4):
                    facc[g, k, a] = zero
            if last:
                for k in range(6):
                    vi[g, k] = zero
                    vj_o[g, k] = zero
                    vj_z[g, k] = zero

        def own_body(c, carry):
            force, _ = tile(0, jof, joi, 1, c, False, 0)
            force_x, total_x = tile(0, jof, joi, 2, c, True, 0)
            add_force(0, [force, force_x])
            for k in range(3):
                jacc_o[0, c, k] = jnp.zeros((8, LANES), jnp.float32)
                jacc_o[1, c, k] = jnp.zeros((8, LANES), jnp.float32)
                jacc_o[2, c, k] = total_x[k]
            if last:
                add_rows(vi, (0,), pair_virial(0, jof, 1, c, force, None))
                part = pair_virial(0, jof, 2, c, force_x, total_x)
                add_rows(vi, (0,), part)
                add_rows(vj_o, (2,), part)
            return carry

        lax.fori_loop(0, C, own_body, 0)

        offset = offsets[step]
        turn_p = jnp.where(iy == ny - 1, offset, 0)
        turn_m = jnp.where(iy == 0, lax.rem(LANES - offset, LANES), 0)
        shear_p = jnp.where(iy == ny - 1, 1.0, 0.0)
        shear_m = jnp.where(iy == 0, -1.0, 0.0)

        def turned(amount):
            return lambda v: jnp.stack([roll(v[a], amount) for a in range(C)])

        send_dn.wait_recv()
        i_prep(
            1, lambda k: jnp.stack([yp[c, k] for c in range(C)]), jnp.stack([yp0[c, 6] for c in range(C)]),
            2.0, shear_p, step, turned(turn_p),
        )

        def multi(g, jf, ji, c, jacc, jat, vj):
            forces = []
            for dxi in range(3):
                force, total = tile(g, jf, ji, dxi, c, True, dxi)
                forces.append(force)
                add_rows(jacc, jat(dxi), total)
                if last:
                    part = pair_virial(g, jf, dxi, c, force, total)
                    add_rows(vi, (g,), part)
                    add_rows(vj, (dxi,), part)
            add_force(g, forces)

        def up_body(c, carry):
            multi(1, jof, joi, c, jacc_o, lambda dxi: (dxi, c), vj_o)
            return carry

        lax.fori_loop(0, C, up_body, 0)

        send_up.wait_recv()
        i_prep(
            2, lambda k: jnp.stack([ym[c, k] for c in range(C)]), jnp.stack([ym0[c, 6] for c in range(C)]),
            -2.0, shear_m, step, turned(turn_m),
        )

        give_z = [remote(rz.at[c], rzm.at[c], step, 6 + c, up_z) for c in range(C)]
        for c in range(C):
            send_z[c].wait_recv()
            j_prep(jzf, c, lambda c, k: zp[c, k], 2.0)
            if not last:
                j_seed(jzi, c, zp0[c, 6])
            for dxi in range(3):
                for k in range(3):
                    jacc_z[dxi, k] = zero

            def z_body(g, carry):
                multi(g, jzf, jzi, c, jacc_z, lambda dxi: (dxi,), vj_z)
                return carry

            lax.fori_loop(0, 3, z_body, 0)
            for k in range(3):
                value = zero
                for dxi in range(3):
                    value = value + back_to_place([jacc_z[dxi, k]], dxi)[0]
                rz[c, k] = value * (-UNIT)
            give_z[c].start()

        scale = UNIT * 0.5 / 8.0

        def virial_rows(ref, at):
            rows = [jnp.sum(ref[at, k], axis=0, keepdims=True) for k in range(6)]
            return jnp.concatenate(rows + [jnp.zeros((2, LANES), jnp.float32)], axis=0) * scale

        undo_p = lax.rem(LANES - turn_p, LANES)
        undo_m = lax.rem(LANES - turn_m, LANES)
        for n, (g, undo) in enumerate(((1, undo_p), (2, undo_m))):
            for k in range(3):
                for a in range(4):
                    ry[n, 4 * k + a] = roll(facc[g, k, a] * UNIT, undo)
            if last:
                ry[n, 12] = roll(virial_rows(vi, g), undo)
        give_up = remote(ry.at[0], rfm, step, 10, up_y)
        give_dn = remote(ry.at[1], rfp, step, 11, dn_y)
        give_up.start()
        give_dn.start()
        if last:
            value = zero
            for dxi in range(3):
                value = value + back_to_place([virial_rows(vj_z, dxi)], dxi)[0]
            vz[...] = value
            give_v = remote(vz, vzm, step, 12, up_z)
            give_v.start()

        mine = [[facc[0, k, a] for a in range(4)] for k in range(3)]
        for dxi in range(3):
            for k in range(3):
                moved = back_to_place([jacc_o[dxi, a, k] for a in range(4)], dxi)
                mine[k] = [mine[k][a] - moved[a] for a in range(4)]
        if last:
            stress = virial_rows(vi, 0)
            for dxi in range(3):
                stress = stress + back_to_place([virial_rows(vj_o, dxi)], dxi)[0]
        give_up.wait_recv()
        give_dn.wait_recv()
        for c in range(C):
            give_z[c].wait_recv()
        for k in range(3):
            for a in range(4):
                total = mine[k][a] * UNIT + rfm[4 * k + a] + rfp[4 * k + a] + rzm[a, k]
                f_out[k, a] = total
                speed = snd[a, 3 + k] + 0.5 * DT * total
                if last:
                    speed = jnp.where(present[a], speed, 0.0)
                else:
                    speed = snd[a, 3 + k]
                v_out[k, a] = speed
        if last:
            give_v.wait_recv()
            s_out[...] = stress + rfm[12] + rfp[12] + vzm[...]
    for copy in started:
        copy.wait_send()


def shards(mesh, positions, velocities, forces_prev, seeds, counts, offsets):
    ny, nz = mesh.shape["xy"], mesh.shape["gz"]
    f32, i32 = jnp.float32, jnp.int32
    vmem = pl.BlockSpec(memory_space=pltpu.VMEM)
    state0, state1 = (C, 7, 8, LANES), (C, 6, 8, LANES)
    scratch = [
        (state0, f32), (state1, f32), (state0, f32), (state1, f32), (state0, f32), (state1, f32),
        (state0, f32), (state1, f32),
        ((2, 12, 8, LANES), f32), ((2, 13, 8, LANES), f32),
        ((C, 3, 8, LANES), f32), ((C, 3, 8, LANES), f32), ((8, LANES), f32),
        ((12, 8, LANES), f32), ((13, 8, LANES), f32), ((12, 8, LANES), f32), ((13, 8, LANES), f32),
        ((C, 3, 8, LANES), f32), ((C, 3, 8, LANES), f32), ((8, LANES), f32),
        ((3, 6, C, 8, LANES), f32), ((3, 2, C, 8, LANES), i32),
        ((3, C, 6, 8, LANES), f32), ((3, C, 2, 8, LANES), i32),
        ((3, C, 6, 8, LANES), f32), ((3, C, 2, 8, LANES), i32),
        ((3, 3, 64, LANES), f32),
        ((3, 3, C, 8, LANES), f32), ((3, C, 3, 8, LANES), f32), ((3, 3, 8, LANES), f32),
        ((3, 6, 8, LANES), f32), ((3, 6, 8, LANES), f32), ((3, 6, 8, LANES), f32),
    ]
    force, speed, stress = pl.pallas_call(
        functools.partial(kernel, ny, nz),
        out_shape=(
            jax.ShapeDtypeStruct((3, C, 8, LANES), f32),
            jax.ShapeDtypeStruct((3, C, 8, LANES), f32),
            jax.ShapeDtypeStruct((8, LANES), f32),
        ),
        in_specs=[vmem] * 5 + [pl.BlockSpec(memory_space=pltpu.SMEM)],
        out_specs=(vmem, vmem, vmem),
        scratch_shapes=[pltpu.VMEM(shape, kind) for shape, kind in scratch]
        + [pltpu.SemaphoreType.DMA((2, 13)), pltpu.SemaphoreType.DMA((2, 13))],
        compiler_params=pltpu.CompilerParams(collective_id=0, has_side_effects=True),
    )(
        positions.reshape(3, C, 8, LANES),
        velocities.reshape(3, C, 8, LANES),
        forces_prev.reshape(3, C, 8, LANES),
        seeds.reshape(C, 8, LANES),
        counts.reshape(1, LANES),
        offsets,
    )
    return (
        force.reshape(3, 4 * 8, 1, 1, LANES),
        speed.reshape(3, 4 * 8, 1, 1, LANES),
        stress[:6].reshape(6, 1, 1, LANES),
    )


def solution(mesh):
    bead = P(None, None, "gz", "xy", None)
    return jax.shard_map(
        functools.partial(shards, mesh),
        mesh=mesh,
        in_specs=(bead, bead, bead, P(None, "gz", "xy", None), P("gz", "xy", None), P()),
        out_specs=(bead, bead, P(None, "gz", "xy", None)),
        check_vma=False,
    )
```

time: 292 us -> 60 us (0.21)
  the two profiles are of different devices: /device:TPU:34 before, /device:TPU:1 now
where the time goes in v1:
time: 60 us; the launch traced here: 59.8 us
  Pallas kernels  55.8 us (93%)
  local copies, waits for them, and re-layouts  3.32 us (6%)
  between operations  0.65 us (1%)
    pallas_call x1, Pallas kernels, shards(): pl.pallas_call(functools.partial(kernel, ny, nz), out_shape=(jax.ShapeDty...  55.8 us
    unnamed x7, local copies, waits for them, and re-layouts  3.31 us

profile of v1, /device:TPU:1, one launch (start us, length us, event | category | flops | bytes accessed | tf_op | source)
XLA Modules:
  0.0 59.8 jit_solution(12074983224149037639)
XLA Ops:
  0.6 55.8 %shard_map.85 = (f32[3,4,8,128]{3,2,1,0:T(8,128)}, f32[3,4,8,128]{3,2,1,0:T(8,128)}, f32[8,128]{1,0:T(8,128)}) custom-call(f32[3,4,8,128]{3,2,1,0:T(8,128)} %bitcast.15, f32[3,4,8,128]{3,2,1,0:T(8,128)} %bitcast.16, f32[3,4,8,128]{3,2,1,0:T(8,128)} %bitcast.17, s32[4,8,128]{2,1,0:T(8,128)} %bitcast.18, s32[1,128]{1,0:T(1,128)} %bitcast.19, s32[2]{0:T(128)} %offsets.1), custom_call_target="tpu_custom_call" | custom-call | tf_op jit(solution)/shard_map/pallas_call | solution.py:374
  56.4 0.0 copy-start.1
  56.4 0.7 %copy-done.1 = f32[8,128]{1,0:T(8,128)S(1)} copy-done((f32[8,128]{1,0:T(8,128)S(1)}, f32[8,128]{1,0:T(8,128)}, u32[]{:S(2)}) %copy-start.1) | copy-done | bytes 4120
  57.1 0.6 copy.11
  57.7 0.0 copy-start
  57.7 1.4 %copy.14 = f32[3,32,1,1,128]{4,3,2,1,0:T(1,128)} copy(f32[3,32,1,1,128]{4,3,2,1,0:T(1,128)} %bitcast.14) | data formatting | bytes 98304
  59.1 0.0 copy-done
  59.1 0.6 %copy.15 = f32[3,32,1,1,128]{4,3,2,1,0:T(1,128)} copy(f32[3,32,1,1,128]{4,3,2,1,0:T(1,128)S(1)} %bitcast.13) | data formatting | bytes 98304
  (1 shorter events, 0.0 us)
Async XLA Ops:
  56.4 0.7 %copy-start.1 = (f32[8,128]{1,0:T(8,128)S(1)}, f32[8,128]{1,0:T(8,128)}, u32[]{:S(2)}) copy-start(f32[8,128]{1,0:T(8,128)} %get-tuple-element.8) | copy-start | bytes 12292
  57.7 1.4 %copy-start = (f32[3,4,8,128]{3,2,1,0:T(8,128)S(1)}, f32[3,4,8,128]{3,2,1,0:T(8,128)}, u32[]{:S(2)}) copy-start(f32[3,4,8,128]{3,2,1,0:T(8,128)} %get-tuple-element.7) | copy-start | bytes 147460

commit v2 on v1

--- a/solution.py
+++ b/solution.py
@@ -31,20 +31,34 @@
 
 
 def kernel(
-    ny, nz, pos, vel, frc, seeds, counts, offsets, f_out, v_out, s_out,
-    snd0, snd1, yp0, yp1, ym0, ym1, zp0, zp1, ry0, ry1, rz0, rz1, vz,
-    rfm0, rfm1, rfp0, rfp1, rzm0, rzm1, vzm,
-    ig, ii, jof, joi, jzf, jzi, gpart, facc, jacc_o, jacc_z, vi, vj_o, vj_z, send, recv,
+    ny, nz, pos_in, vel_in, frc_in, seeds_in, counts_in, offsets_in, f_out, v_out, s_out,
+    pos, vel, frc, seeds, counts, offsets, load,
+    snd0, snd1, yn0, yn1, yf0, yf1, zp0, zp1, zm0, zm1, ry0, ry1, rz0, rz1, vz,
+    rfn0, rfn1, rff0, rff1, rzm0, rzm1, vzm,
+    ig, ii, jof, joi, jzf, jzi, jmf, jmi, gpart, facc, jacc_o, jacc_z, vi, vj_o, vj_z, send, recv,
 ):
     iy = lax.axis_index("xy")
     iz = lax.axis_index("gz")
-    up_y = {"xy": lax.rem(iy + 1, ny), "gz": iz}
-    dn_y = {"xy": lax.rem(iy + ny - 1, ny), "gz": iz}
+    odd = lax.rem(iy, 2)
+    side = 1.0 - 2.0 * odd.astype(jnp.float32)
+    near_y = {"xy": iy + 1 - 2 * odd, "gz": iz}
+    far_y = {"xy": lax.rem(iy + ny - 1 + 2 * odd, ny), "gz": iz}
     up_z = {"xy": iy, "gz": lax.rem(iz + 1, nz)}
     dn_z = {"xy": iy, "gz": lax.rem(iz + nz - 1, nz)}
     barrier = pltpu.get_barrier_semaphore()
-    for where in (up_y, dn_y, up_z, dn_z):
+    for where in (near_y, far_y, up_z, dn_z):
         pl.semaphore_signal(barrier, inc=1, device_id=where, device_id_type=pl.DeviceIdType.MESH)
+
+    loads = [
+        pltpu.make_async_copy(src, dst, load.at[n])
+        for n, (src, dst) in enumerate(
+            ((vel_in, vel), (frc_in, frc), (pos_in, pos), (counts_in, counts), (seeds_in, seeds), (offsets_in, offsets))
+        )
+    ]
+    for copy in loads:
+        copy.start()
+    for copy in loads[:5]:
+        copy.wait()
 
     started = []
 
@@ -61,14 +75,14 @@
     )
     present = slot_no < counts[...]
 
-    def tile(g, jf, ji, dxi, c, react, at):
-        force = [[jnp.zeros((8, LANES), jnp.float32) for _ in range(4)] for _ in range(3)]
+    def tile(g, jf, ji, dxi, c, react, at, rows=range(4)):
+        force = [{a: jnp.zeros((8, LANES), jnp.float32) for a in rows} for _ in range(3)]
         for j in range(8):
             near = [jnp.broadcast_to(jf[dxi, c, k, j : j + 1, :], (8, LANES)) for k in range(6)]
             seed_j = jnp.broadcast_to(ji[dxi, c, 0, j : j + 1, :], (8, LANES))
             base_j = jnp.broadcast_to(ji[dxi, c, 1, j : j + 1, :], (8, LANES))
             back = [None, None, None]
-            for a in range(4):
+            for a in rows:
                 d = [ig[g, k, a] - near[k] for k in range(3)]
                 u = [ig[g, 3 + k, a] - near[3 + k] for k in range(3)]
                 square = d[0] * d[0] + d[1] * d[1] + d[2] * d[2]
@@ -89,17 +103,17 @@
         if react:
             total = []
             for k in range(3):
-                rows = [gpart[at, k, pl.ds(s, 8, stride=8), :] for s in range(8)]
-                while len(rows) > 1:
-                    rows = [rows[i] + rows[i + 1] for i in range(0, len(rows), 2)]
-                total.append(rows[0])
+                sums = [gpart[at, k, pl.ds(s, 8, stride=8), :] for s in range(8)]
+                while len(sums) > 1:
+                    sums = [sums[i] + sums[i + 1] for i in range(0, len(sums), 2)]
+                total.append(sums[0])
         return force, total
 
     def pair_virial(g, jf, dxi, c, force, total):
         out = []
         for first, second in PAIRS:
             part = None
-            for a in range(4):
+            for a in force[second]:
                 term = ig[g, first, a] * force[second][a]
                 part = term if part is None else part + term
             if total is None:
@@ -111,7 +125,7 @@
 
     def add_force(g, forces):
         for k in range(3):
-            for a in range(4):
+            for a in forces[0][k]:
                 value = facc[g, k, a]
                 for force in forces:
                     value = value + force[k][a]
@@ -124,7 +138,7 @@
     def i_prep(g, block, seed, shift_y, shear, step, turn):
         for k in range(3):
             value = turn(block(k))
-            if k == 1 and shift_y != 0.0:
+            if k == 1 and shift_y is not None:
                 value = value + shift_y
             for a in range(4):
                 ig[g, k, a] = value[a]
@@ -169,8 +183,8 @@
 
     for step in range(2):
         last = step == 1
-        snd, yp, ym, zp = (snd1, yp1, ym1, zp1) if last else (snd0, yp0, ym0, zp0)
-        ry, rz, rfm, rfp, rzm = (ry1, rz1, rfm1, rfp1, rzm1) if last else (ry0, rz0, rfm0, rfp0, rzm0)
+        snd, yn, yf, zp, zm = (snd1, yn1, yf1, zp1, zm1) if last else (snd0, yn0, yf0, zp0, zm0)
+        ry, rz, rfn, rff, rzm = (ry1, rz1, rfn1, rff1, rzm1) if last else (ry0, rz0, rfn0, rff0, rzm0)
         for k in range(3):
             if not last:
                 half = vel[k] + 0.5 * DT * frc[k]
@@ -191,17 +205,18 @@
             return jnp.stack([snd[c, k] for c in range(C)])
 
         seed_own = jnp.stack([snd0[c, 6] for c in range(C)])
-        i_prep(0, own, seed_own, 0.0, None, step, lambda v: v)
+        i_prep(0, own, seed_own, None, None, step, lambda v: v)
         if not last:
             pl.semaphore_wait(barrier, 4)
         send_z = [remote(snd.at[c], zp.at[c], step, c, dn_z) for c in range(C)]
-        send_up = remote(snd, ym, step, 4, up_y)
-        send_dn = remote(snd, yp, step, 5, dn_y)
-        send_z[0].start()
-        send_dn.start()
-        send_up.start()
-        for c in range(1, C):
+        send_near = remote(snd, yn, step, 4, near_y)
+        send_far = remote(snd, yf, step, 5, far_y)
+        send_near.start()
+        for c in range(C):
             send_z[c].start()
+        send_far.start()
+        send_lower = remote(snd.at[pl.ds(2, 2)], zm, step, 13, up_z)
+        send_lower.start()
 
         for c in range(C):
             j_prep(jof, c, lambda c, k: snd[c, k], 0.0)
@@ -235,85 +250,108 @@
 
         lax.fori_loop(0, C, own_body, 0)
 
-        offset = offsets[step]
-        turn_p = jnp.where(iy == ny - 1, offset, 0)
-        turn_m = jnp.where(iy == 0, lax.rem(LANES - offset, LANES), 0)
-        shear_p = jnp.where(iy == ny - 1, 1.0, 0.0)
-        shear_m = jnp.where(iy == 0, -1.0, 0.0)
-
-        def turned(amount):
-            return lambda v: jnp.stack([roll(v[a], amount) for a in range(C)])
-
-        send_dn.wait_recv()
-        i_prep(
-            1, lambda k: jnp.stack([yp[c, k] for c in range(C)]), jnp.stack([yp0[c, 6] for c in range(C)]),
-            2.0, shear_p, step, turned(turn_p),
-        )
-
-        def multi(g, jf, ji, c, jacc, jat, vj):
+        def multi(g, jf, ji, c, jacc, vj, rows=range(4)):
             forces = []
             for dxi in range(3):
-                force, total = tile(g, jf, ji, dxi, c, True, dxi)
+                force, total = tile(g, jf, ji, dxi, c, last or jacc is not None, dxi, rows)
                 forces.append(force)
-                add_rows(jacc, jat(dxi), total)
+                if jacc is not None:
+                    add_rows(jacc, (dxi, c), total)
                 if last:
                     part = pair_virial(g, jf, dxi, c, force, total)
                     add_rows(vi, (g,), part)
-                    add_rows(vj, (dxi,), part)
+                    if vj is not None:
+                        add_rows(vj, (dxi,), part)
             add_force(g, forces)
 
-        def up_body(c, carry):
-            multi(1, jof, joi, c, jacc_o, lambda dxi: (dxi, c), vj_o)
-            return carry
-
-        lax.fori_loop(0, C, up_body, 0)
-
-        send_up.wait_recv()
+        def pair_own(g):
+            def body(c, carry):
+                multi(g, jof, joi, c, jacc_o, vj_o)
+                return carry
+
+            lax.fori_loop(0, C, body, 0)
+
+        def pair_z(jf, ji, chunks, rows):
+            def body(c, carry):
+                multi(0, jf, ji, c, None, None, rows)
+                return carry
+
+            lax.fori_loop(0, chunks, body, 0)
+
+        scale = UNIT * 0.5 / 8.0
+
+        def virial_rows(ref, at):
+            rows = [jnp.sum(ref[at, k], axis=0, keepdims=True) for k in range(6)]
+            return jnp.concatenate(rows + [jnp.zeros((2, LANES), jnp.float32)], axis=0) * scale
+
+        send_near.wait_recv()
         i_prep(
-            2, lambda k: jnp.stack([ym[c, k] for c in range(C)]), jnp.stack([ym0[c, 6] for c in range(C)]),
-            -2.0, shear_m, step, turned(turn_m),
+            1, lambda k: jnp.stack([yn[c, k] for c in range(C)]), jnp.stack([yn0[c, 6] for c in range(C)]),
+            2.0 * side, None, step, lambda v: v,
         )
 
-        give_z = [remote(rz.at[c], rzm.at[c], step, 6 + c, up_z) for c in range(C)]
-        for c in range(C):
-            send_z[c].wait_recv()
+        @pl.when(odd == 0)
+        def _():
+            pair_own(1)
+
+        def near_body(c, carry):
+            pltpu.make_async_remote_copy(
+                src_ref=snd.at[c], dst_ref=zp.at[c], send_sem=send.at[step, c], recv_sem=recv.at[step, c],
+                device_id=dn_z, device_id_type=pl.DeviceIdType.MESH,
+            ).wait_recv()
             j_prep(jzf, c, lambda c, k: zp[c, k], 2.0)
             if not last:
                 j_seed(jzi, c, zp0[c, 6])
             for dxi in range(3):
                 for k in range(3):
-                    jacc_z[dxi, k] = zero
-
-            def z_body(g, carry):
-                multi(g, jzf, jzi, c, jacc_z, lambda dxi: (dxi,), vj_z)
-                return carry
-
-            lax.fori_loop(0, 3, z_body, 0)
+                    jacc_z[dxi, c, k] = zero
+            multi(1, jzf, jzi, c, jacc_z, vj_z)
+            multi(0, jzf, jzi, c, jacc_z, vj_z, (0, 1))
+            return carry
+
+        lax.fori_loop(0, C, near_body, 0)
+
+        for k in range(3):
+            for a in range(4):
+                ry[0, 4 * k + a] = facc[1, k, a] * UNIT
+        if last:
+            ry[0, 12] = virial_rows(vi, 1)
+        give_near = remote(ry.at[0], rfn, step, 10, near_y)
+        give_near.start()
+
+        if not last:
+            loads[5].wait()
+        offset = offsets[step]
+        top = iy == ny - 1
+        bottom = iy == 0
+        turn = jnp.where(top, offset, jnp.where(bottom, lax.rem(LANES - offset, LANES), 0))
+        undo = lax.rem(LANES - turn, LANES)
+        shear = jnp.where(top, 1.0, jnp.where(bottom, -1.0, 0.0))
+        send_far.wait_recv()
+        i_prep(
+            2, lambda k: jnp.stack([yf[c, k] for c in range(C)]), jnp.stack([yf0[c, 6] for c in range(C)]),
+            -2.0 * side, shear, step, lambda v: jnp.stack([roll(v[a], turn) for a in range(C)]),
+        )
+
+        def give_chunk(c):
+            return pltpu.make_async_remote_copy(
+                src_ref=rz.at[c], dst_ref=rzm.at[c], send_sem=send.at[step, 6 + c], recv_sem=recv.at[step, 6 + c],
+                device_id=up_z, device_id_type=pl.DeviceIdType.MESH,
+            )
+
+        def far_body(c, carry):
+            multi(2, jzf, jzi, c, jacc_z, vj_z)
             for k in range(3):
                 value = zero
                 for dxi in range(3):
-                    value = value + back_to_place([jacc_z[dxi, k]], dxi)[0]
+                    value = value + back_to_place([jacc_z[dxi, c, k]], dxi)[0]
                 rz[c, k] = value * (-UNIT)
-            give_z[c].start()
-
-        scale = UNIT * 0.5 / 8.0
-
-        def virial_rows(ref, at):
-            rows = [jnp.sum(ref[at, k], axis=0, keepdims=True) for k in range(6)]
-            return jnp.concatenate(rows + [jnp.zeros((2, LANES), jnp.float32)], axis=0) * scale
-
-        undo_p = lax.rem(LANES - turn_p, LANES)
-        undo_m = lax.rem(LANES - turn_m, LANES)
-        for n, (g, undo) in enumerate(((1, undo_p), (2, undo_m))):
-            for k in range(3):
-                for a in range(4):
-                    ry[n, 4 * k + a] = roll(facc[g, k, a] * UNIT, undo)
-            if last:
-                ry[n, 12] = roll(virial_rows(vi, g), undo)
-        give_up = remote(ry.at[0], rfm, step, 10, up_y)
-        give_dn = remote(ry.at[1], rfp, step, 11, dn_y)
-        give_up.start()
-        give_dn.start()
+            give_chunk(c).start()
+            return carry
+
+        lax.fori_loop(0, C, far_body, 0)
+        give_z = [give_chunk(c) for c in range(C)]
+        started.extend(give_z)
         if last:
             value = zero
             for dxi in range(3):
@@ -321,6 +359,26 @@
             vz[...] = value
             give_v = remote(vz, vzm, step, 12, up_z)
             give_v.start()
+
+        @pl.when(odd == 1)
+        def _():
+            pair_own(2)
+
+        for k in range(3):
+            for a in range(4):
+                ry[1, 4 * k + a] = roll(facc[2, k, a] * UNIT, undo)
+        if last:
+            ry[1, 12] = roll(virial_rows(vi, 2), undo)
+        give_far = remote(ry.at[1], rff, step, 11, far_y)
+        give_far.start()
+
+        pair_z(jzf, jzi, C, (2, 3))
+        send_lower.wait_recv()
+        for c in range(2):
+            j_prep(jmf, c, lambda c, k: zm[c, k], -2.0)
+            if not last:
+                j_seed(jmi, c, zm0[c, 6])
+        pair_z(jmf, jmi, 2, range(4))
 
         mine = [[facc[0, k, a] for a in range(4)] for k in range(3)]
         for dxi in range(3):
@@ -331,13 +389,13 @@
             stress = virial_rows(vi, 0)
             for dxi in range(3):
                 stress = stress + back_to_place([virial_rows(vj_o, dxi)], dxi)[0]
-        give_up.wait_recv()
-        give_dn.wait_recv()
+        give_near.wait_recv()
         for c in range(C):
             give_z[c].wait_recv()
+        give_far.wait_recv()
         for k in range(3):
             for a in range(4):
-                total = mine[k][a] * UNIT + rfm[4 * k + a] + rfp[4 * k + a] + rzm[a, k]
+                total = mine[k][a] * UNIT + rfn[4 * k + a] + rff[4 * k + a] + rzm[a, k]
                 f_out[k, a] = total
                 speed = snd[a, 3 + k] + 0.5 * DT * total
                 if last:
@@ -347,7 +405,9 @@
                 v_out[k, a] = speed
         if last:
             give_v.wait_recv()
-            s_out[...] = stress + rfm[12] + rfp[12] + vzm[...]
+            stress = stress + rfn[12] + rff[12] + vzm[...]
+            for k in range(6):
+                s_out[k] = stress[k : k + 1, :]
     for copy in started:
         copy.wait_send()
 
@@ -357,9 +417,8 @@
     f32, i32 = jnp.float32, jnp.int32
     vmem = pl.BlockSpec(memory_space=pltpu.VMEM)
     state0, state1 = (C, 7, 8, LANES), (C, 6, 8, LANES)
-    scratch = [
-        (state0, f32), (state1, f32), (state0, f32), (state1, f32), (state0, f32), (state1, f32),
-        (state0, f32), (state1, f32),
+    bead = (3, C, 8, LANES)
+    scratch = [(state0, f32), (state1, f32)] * 4 + [((2, 7, 8, LANES), f32), ((2, 6, 8, LANES), f32)] + [
         ((2, 12, 8, LANES), f32), ((2, 13, 8, LANES), f32),
         ((C, 3, 8, LANES), f32), ((C, 3, 8, LANES), f32), ((8, LANES), f32),
         ((12, 8, LANES), f32), ((13, 8, LANES), f32), ((12, 8, LANES), f32), ((13, 8, LANES), f32),
@@ -367,26 +426,26 @@
         ((3, 6, C, 8, LANES), f32), ((3, 2, C, 8, LANES), i32),
         ((3, C, 6, 8, LANES), f32), ((3, C, 2, 8, LANES), i32),
         ((3, C, 6, 8, LANES), f32), ((3, C, 2, 8, LANES), i32),
+        ((3, C, 6, 8, LANES), f32), ((3, C, 2, 8, LANES), i32),
         ((3, 3, 64, LANES), f32),
-        ((3, 3, C, 8, LANES), f32), ((3, C, 3, 8, LANES), f32), ((3, 3, 8, LANES), f32),
+        ((3, 3, C, 8, LANES), f32), ((3, C, 3, 8, LANES), f32), ((3, C, 3, 8, LANES), f32),
         ((3, 6, 8, LANES), f32), ((3, 6, 8, LANES), f32), ((3, 6, 8, LANES), f32),
     ]
+    inputs = [(bead, f32), (bead, f32), (bead, f32), ((C, 8, LANES), i32), ((1, LANES), i32)]
     force, speed, stress = pl.pallas_call(
         functools.partial(kernel, ny, nz),
-        out_shape=(
-            jax.ShapeDtypeStruct((3, C, 8, LANES), f32),
-            jax.ShapeDtypeStruct((3, C, 8, LANES), f32),
-            jax.ShapeDtypeStruct((8, LANES), f32),
-        ),
-        in_specs=[vmem] * 5 + [pl.BlockSpec(memory_space=pltpu.SMEM)],
+        out_shape=(pltpu.VMEM(bead, f32), pltpu.VMEM(bead, f32), pltpu.VMEM((6, 1, LANES), f32)),
+        in_specs=[pl.BlockSpec(memory_space=pl.ANY)] * 6,
         out_specs=(vmem, vmem, vmem),
-        scratch_shapes=[pltpu.VMEM(shape, kind) for shape, kind in scratch]
-        + [pltpu.SemaphoreType.DMA((2, 13)), pltpu.SemaphoreType.DMA((2, 13))],
+        scratch_shapes=[pltpu.VMEM(shape, kind) for shape, kind in inputs]
+        + [pltpu.SMEM((2,), i32), pltpu.SemaphoreType.DMA((6,))]
+        + [pltpu.VMEM(shape, kind) for shape, kind in scratch]
+        + [pltpu.SemaphoreType.DMA((2, 14)), pltpu.SemaphoreType.DMA((2, 14))],
         compiler_params=pltpu.CompilerParams(collective_id=0, has_side_effects=True),
     )(
-        positions.reshape(3, C, 8, LANES),
-        velocities.reshape(3, C, 8, LANES),
-        forces_prev.reshape(3, C, 8, LANES),
+        positions.reshape(bead),
+        velocities.reshape(bead),
+        forces_prev.reshape(bead),
         seeds.reshape(C, 8, LANES),
         counts.reshape(1, LANES),
         offsets,
@@ -394,7 +453,7 @@
     return (
         force.reshape(3, 4 * 8, 1, 1, LANES),
         speed.reshape(3, 4 * 8, 1, 1, LANES),
-        stress[:6].reshape(6, 1, 1, LANES),
+        stress.reshape(6, 1, 1, LANES),
     )
 
 

time: 60 us -> 56.3 us (0.938)
  the two profiles are of different devices: /device:TPU:1 before, /device:TPU:32 now
where the time goes in v2:
time: 56.3 us; the launch traced here: 56.1 us
  Pallas kernels  53.7 us (95%)
  local copies, waits for them, and re-layouts  1.82 us (3%)
  between operations  0.64 us (1%)
    pallas_call x1, Pallas kernels, shards(): pl.pallas_call(functools.partial(kernel, ny, nz), out_shape=(pltpu.VMEM(b...  53.7 us
    unnamed x3, local copies, waits for them, and re-layouts  1.82 us

profile of v2, /device:TPU:32, one launch (start us, length us, event | category | flops | bytes accessed | tf_op | source)
XLA Modules:
  0.0 56.1 jit_solution(11107025609405409438)
XLA Ops:
  0.6 53.7 %shard_map.85 = (f32[3,4,8,128]{3,2,1,0:T(8,128)S(1)}, f32[3,4,8,128]{3,2,1,0:T(8,128)S(1)}, f32[6,1,128]{2,1,0:T(1,128)S(1)}) custom-call(f32[3,4,8,128]{3,2,1,0:T(8,128)} %bitcast.17, f32[3,4,8,128]{3,2,1,0:T(8,128)} %bitcast.18, f32[3,4,8,128]{3,2,1,0:T(8,128)} %bitcast.19, s32[4,8,128]{2,1,0:T(8,128)} %bitcast.20, s32[1,128]{1,0:T(1,128)} %bitcast.21, ...), custom_call_target="tpu_custom_call" | custom-call | tf_op jit(solution)/shard_map/pallas_call | solution.py:435
  54.3 0.6 %copy.15 = f32[3,32,1,1,128]{4,3,2,1,0:T(1,128)} copy(f32[3,32,1,1,128]{4,3,2,1,0:T(1,128)S(1)} %bitcast.15) | data formatting | bytes 98304
  54.9 0.6 %copy.16 = f32[3,32,1,1,128]{4,3,2,1,0:T(1,128)} copy(f32[3,32,1,1,128]{4,3,2,1,0:T(1,128)S(1)} %bitcast.14) | data formatting | bytes 98304
  55.6 0.6 %copy.17 = f32[6,1,1,128]{3,2,1,0:T(1,128)} copy(f32[6,1,1,128]{3,2,1,0:T(1,128)S(1)} %bitcast.16) | data formatting | bytes 6144

commit v3 on v2

--- a/solution.py
+++ b/solution.py
@@ -61,6 +61,7 @@
         copy.wait()
 
     started = []
+    lowers = []
 
     def remote(src, dst, step, slot, where):
         copy = pltpu.make_async_remote_copy(
@@ -215,8 +216,16 @@
         for c in range(C):
             send_z[c].start()
         send_far.start()
-        send_lower = remote(snd.at[pl.ds(2, 2)], zm, step, 13, up_z)
-        send_lower.start()
+        send_lower = pltpu.make_async_remote_copy(
+            src_ref=snd, dst_ref=zm, send_sem=send.at[step, 13], recv_sem=recv.at[step, 13],
+            device_id=up_z, device_id_type=pl.DeviceIdType.MESH,
+        )
+        lowers.append(send_lower)
+
+        @pl.when(odd == 0)
+        def _():
+            send_lower.start()
+
 
         for c in range(C):
             j_prep(jof, c, lambda c, k: snd[c, k], 0.0)
@@ -271,12 +280,12 @@
 
             lax.fori_loop(0, C, body, 0)
 
-        def pair_z(jf, ji, chunks, rows):
+        def pair_z(jf, ji):
             def body(c, carry):
-                multi(0, jf, ji, c, None, None, rows)
+                multi(0, jf, ji, c, None, None)
                 return carry
 
-            lax.fori_loop(0, chunks, body, 0)
+            lax.fori_loop(0, C, body, 0)
 
         scale = UNIT * 0.5 / 8.0
 
@@ -294,7 +303,7 @@
         def _():
             pair_own(1)
 
-        def near_body(c, carry):
+        def near_body(both, c, carry):
             pltpu.make_async_remote_copy(
                 src_ref=snd.at[c], dst_ref=zp.at[c], send_sem=send.at[step, c], recv_sem=recv.at[step, c],
                 device_id=dn_z, device_id_type=pl.DeviceIdType.MESH,
@@ -306,10 +315,17 @@
                 for k in range(3):
                     jacc_z[dxi, c, k] = zero
             multi(1, jzf, jzi, c, jacc_z, vj_z)
-            multi(0, jzf, jzi, c, jacc_z, vj_z, (0, 1))
+            if both:
+                multi(0, jzf, jzi, c, jacc_z, vj_z)
             return carry
 
-        lax.fori_loop(0, C, near_body, 0)
+        @pl.when(odd == 0)
+        def _():
+            lax.fori_loop(0, C, functools.partial(near_body, False), 0)
+
+        @pl.when(odd == 1)
+        def _():
+            lax.fori_loop(0, C, functools.partial(near_body, True), 0)
 
         for k in range(3):
             for a in range(4):
@@ -372,13 +388,15 @@
         give_far = remote(ry.at[1], rff, step, 11, far_y)
         give_far.start()
 
-        pair_z(jzf, jzi, C, (2, 3))
-        send_lower.wait_recv()
-        for c in range(2):
-            j_prep(jmf, c, lambda c, k: zm[c, k], -2.0)
-            if not last:
-                j_seed(jmi, c, zm0[c, 6])
-        pair_z(jmf, jmi, 2, range(4))
+        @pl.when(odd == 0)
+        def _():
+            pair_z(jzf, jzi)
+            send_lower.wait_recv()
+            for c in range(C):
+                j_prep(jmf, c, lambda c, k: zm[c, k], -2.0)
+                if not last:
+                    j_seed(jmi, c, zm0[c, 6])
+            pair_z(jmf, jmi)
 
         mine = [[facc[0, k, a] for a in range(4)] for k in range(3)]
         for dxi in range(3):
@@ -411,6 +429,11 @@
     for copy in started:
         copy.wait_send()
 
+    @pl.when(odd == 0)
+    def _():
+        for copy in lowers:
+            copy.wait_send()
+
 
 def shards(mesh, positions, velocities, forces_prev, seeds, counts, offsets):
     ny, nz = mesh.shape["xy"], mesh.shape["gz"]
@@ -418,7 +441,7 @@
     vmem = pl.BlockSpec(memory_space=pltpu.VMEM)
     state0, state1 = (C, 7, 8, LANES), (C, 6, 8, LANES)
     bead = (3, C, 8, LANES)
-    scratch = [(state0, f32), (state1, f32)] * 4 + [((2, 7, 8, LANES), f32), ((2, 6, 8, LANES), f32)] + [
+    scratch = [(state0, f32), (state1, f32)] * 5 + [
         ((2, 12, 8, LANES), f32), ((2, 13, 8, LANES), f32),
         ((C, 3, 8, LANES), f32), ((C, 3, 8, LANES), f32), ((8, LANES), f32),
         ((12, 8, LANES), f32), ((13, 8, LANES), f32), ((12, 8, LANES), f32), ((13, 8, LANES), f32),

time: 56.3 us -> 55.6 us (0.988)
  the two profiles are of different devices: /device:TPU:32 before, /device:TPU:1 now
where the time goes in v3:
time: 55.6 us; the launch traced here: 54.8 us
  Pallas kernels  52.4 us (94%)
  local copies, waits for them, and re-layouts  1.82 us (3%)
  between operations  0.64 us (1%)
    pallas_call x1, Pallas kernels, shards(): pl.pallas_call(functools.partial(kernel, ny, nz), out_shape=(pltpu.VMEM(b...  52.4 us
    unnamed x3, local copies, waits for them, and re-layouts  1.82 us

profile of v3, /device:TPU:1, one launch (start us, length us, event | category | flops | bytes accessed | tf_op | source)
XLA Modules:
  0.0 54.8 jit_solution(11882213739831809076)
XLA Ops:
  0.6 52.4 %shard_map.85 = (f32[3,4,8,128]{3,2,1,0:T(8,128)S(1)}, f32[3,4,8,128]{3,2,1,0:T(8,128)S(1)}, f32[6,1,128]{2,1,0:T(1,128)S(1)}) custom-call(f32[3,4,8,128]{3,2,1,0:T(8,128)} %bitcast.17, f32[3,4,8,128]{3,2,1,0:T(8,128)} %bitcast.18, f32[3,4,8,128]{3,2,1,0:T(8,128)} %bitcast.19, s32[4,8,128]{2,1,0:T(8,128)} %bitcast.20, s32[1,128]{1,0:T(1,128)} %bitcast.21, ...), custom_call_target="tpu_custom_call" | custom-call | tf_op jit(solution)/shard_map/pallas_call | solution.py:458
  53.0 0.6 %copy.15 = f32[3,32,1,1,128]{4,3,2,1,0:T(1,128)} copy(f32[3,32,1,1,128]{4,3,2,1,0:T(1,128)S(1)} %bitcast.15) | data formatting | bytes 98304
  53.6 0.6 %copy.16 = f32[3,32,1,1,128]{4,3,2,1,0:T(1,128)} copy(f32[3,32,1,1,128]{4,3,2,1,0:T(1,128)S(1)} %bitcast.14) | data formatting | bytes 98304
  54.2 0.6 %copy.17 = f32[6,1,1,128]{3,2,1,0:T(1,128)} copy(f32[6,1,1,128]{3,2,1,0:T(1,128)S(1)} %bitcast.16) | data formatting | bytes 6144
